TPU v7x, 256 devices: a whole 4x4x8 slice. The times are simulated.
256 devices in a mesh: grp: 8 (over x_lo, y), smp: 32 (over x_hi, z, core).
Axes of the slice: x: 4 (x_hi: 2, x_lo: 2; x = x_hi * 2 + x_lo), y: 4, z: 8, core: 2. Of those that a mesh axis runs over, the one named last changes fastest.
Arguments:
- spins_packed: int32 [32, 32768], P(None, 'smp'), may hold values from -2147483648 to 2147483646
- weight: bfloat16 [1024, 8192], P(None, 'grp'), may hold values from -0.1875 to 0.1875
- hidden_bias: float32 [8192], P('grp'), may hold values from -1.5 to 1.5
- force_w: float32 [1024, 8192], P('smp', 'grp'), may hold values from -6 to 6
- force_b: float32 [8192], P('grp'), may hold values from -6 to 6
Outputs:
- update_w: float32 [1024, 8192], P('smp', 'grp')
- update_b: float32 [8192], P('grp')
All inputs are finite; a program needn't handle non-finite values.
Results may differ from a plain program's by a relative error of at most 0.0003.
Values sent between devices are 32-bit elements; how exact they have to be, the bound alone decides.
A program may use at most 64 MiB of HBM per device.

v0:
```python
import functools

import jax
import jax.numpy as jnp
from jax import lax
from jax.sharding import Mesh
from jax.sharding import PartitionSpec as P

ITERS = 2
GRP = ("grp_0", "grp_1")
SMP = ("smp_0", "smp_1", "smp_2")
GRP_SMP = ("grp_0", "grp_1", "smp_0", "smp_1", "smp_2")


diag_shift = 0.01


def one_axis_at_a_time(value, axes):
    return functools.reduce(lax.psum, axes, value)


def joined_along(tiles, dim):
    shape = list(tiles.shape[1:])
    shape[dim] *= tiles.shape[0]
    return jnp.moveaxis(tiles, 0, dim).reshape(shape)


def all_blocks(value, axes, order):
    tiles = value
    for k in order:
        tiles = lax.all_gather(tiles, axes[k])
    done = order[::-1]
    back = [done.index(k) for k in range(len(axes))]
    tiles = tiles.transpose(*back, *range(len(axes), tiles.ndim))
    return tiles.reshape(-1, *value.shape)


def gather_axes(value, axes, order, dim):
    return joined_along(all_blocks(value, axes, order), dim)


def sent_to_all(value, axis):
    size = lax.axis_size(axis)
    return lax.all_to_all(
        jnp.broadcast_to(value[None], (size, *value.shape)), axis, 0, 0, tiled=True
    )


def over_copies(value, axis):
    return sent_to_all(value, axis).sum(axis=0)


def unpack(packed):
    shifts = jnp.arange(32, dtype=jnp.int32)
    bit_values = jnp.bitwise_and(jnp.right_shift(packed[:, None, :], shifts[None, :, None]), 1)
    signs = 2 * bit_values - 1
    return signs.reshape(packed.shape[0] * 32, packed.shape[1]).astype(jnp.bfloat16)


def body(spins_packed, weight, hidden_bias, force_w, force_b):
    group_size = lax.axis_size(GRP)
    shard_size = lax.axis_size(SMP)
    spins = unpack(spins_packed)
    sample_count = spins.shape[1] * shard_size
    pre_activation = jnp.einsum("it,ih->th", spins, weight, preferred_element_type=jnp.float32)
    hidden = jnp.tanh(pre_activation + hidden_bias)

    def vector_dot(first_w, first_b, second_w, second_b):
        local_sum = jnp.sum(first_w * second_w) + jnp.sum(first_b * second_b) / shard_size
        return one_axis_at_a_time(local_sum, GRP_SMP)

    solution_w = jnp.zeros_like(force_w)
    solution_b = jnp.zeros_like(force_b)
    residual_w, residual_b = (force_w, force_b)
    direction_w, direction_b = (force_w, force_b)
    norm_now = vector_dot(residual_w, residual_b, residual_w, residual_b)
    for iteration in range(ITERS):
        final_turn = iteration + 1 == ITERS
        projected = jnp.einsum(
            "it,ih->th",
            spins,
            gather_axes(direction_w, SMP, (0, 1, 2), 0),
            precision=lax.Precision.HIGHEST,
            preferred_element_type=jnp.float32,
        )
        partial_value = jnp.sum(hidden * (projected + direction_b), axis=1)
        sample_values = over_copies(partial_value, GRP)
        mean_value = over_copies(jnp.sum(sample_values), SMP) / sample_count
        centred = sample_values - mean_value
        local_sum = jnp.sum(centred * centred) / (sample_count * group_size)
        local_sum = local_sum + diag_shift * (
            jnp.sum(direction_w * direction_w) + jnp.sum(direction_b * direction_b) / shard_size
        )
        curvature = one_axis_at_a_time(local_sum, GRP_SMP)
        if not final_turn:
            scaled = centred / sample_count
            weighted = scaled[:, None] * hidden
            image_w = (
                lax.psum_scatter(
                    jnp.einsum(
                        "it,th->ih",
                        spins,
                        weighted,
                        precision=lax.Precision.HIGHEST,
                        preferred_element_type=jnp.float32,
                    ),
                    SMP,
                    scatter_dimension=0,
                    tiled=True,
                )
                + diag_shift * direction_w
            )
            bias_term = jnp.dot(
                scaled, hidden, precision=lax.Precision.HIGHEST, preferred_element_type=jnp.float32
            )
            image_b = over_copies(bias_term, SMP) + diag_shift * direction_b
            image_w, image_b = (image_w, image_b)
        step_size = norm_now / curvature
        solution_w = solution_w + step_size * direction_w
        solution_b = solution_b + step_size * direction_b
        if not final_turn:
            residual_w = residual_w - step_size * image_w
            residual_b = residual_b - step_size * image_b
            norm_next = vector_dot(residual_w, residual_b, residual_w, residual_b)
            direction_w = residual_w + norm_next / norm_now * direction_w
            direction_b = residual_b + norm_next / norm_now * direction_b
            norm_now = norm_next
    return (solution_w, solution_b)


def solution(mesh):
    torus = Mesh(mesh.devices.reshape(2, 4, 2, 8, 2), ("grp_0", "grp_1", "smp_0", "smp_1", "smp_2"))
    in_specs = (P(None, SMP), P(None, GRP), P(GRP), P(SMP, GRP), P(GRP))
    out_specs = (P(SMP, GRP), P(GRP))
    return jax.shard_map(body, mesh=torus, in_specs=in_specs, out_specs=out_specs, check_vma=False)
```

profile of v0, /device:TPU:1, one launch (start us, length us, event | category | flops | bytes accessed | tf_op | source)
XLA Modules:
  0.0 466.7 jit_solution(8668620236048288955)
XLA Ops:
  7.2 8.6 %all-gather = f32[64,1024]{1,0:T(8,128)} all-gather(f32[32,1024]{1,0:T(8,128)} %param.8), channel_id=2, replica_groups=mesh['grp_0'=2,'grp_1'=4,'smp_0'=2,'smp_1'=8,'smp_2'=2] {'smp_0'}, dimensions={0}, use_global_device_ids=true | all-gather | bytes 393216 | tf_op jit(solution)/shard_map/all_gather | solution.py:31
  15.8 0.0 all-gather.13.cloned.1.call-start
  15.9 39.8 %all-gather.11.cloned.1.call-done = f32[16,32,1024]{2,1,0:T(8,128)} async-done(((f32[2,32,1024]{2,1,0:T(8,128)}), f32[16,32,1024]{2,1,0:T(8,128)}) %all-gather.11.cloned.1.call-update) | async-done | bytes 2097168 | tf_op jit(solution)/shard_map/all_gather | solution.py:31
  55.8 0.0 reduce-scatter.2.cloned.1.call-start
  55.8 0.1 shift_right_arithmetic.38
  55.9 1.7 fusion.3
  57.6 2.3 add_convert_fusion
  60.0 4.3 fusion.12
  64.3 15.7 %all-gather.13.cloned.1.call-done = f32[16,2,32,1024]{3,2,1,0:T(8,128)} async-done(((f32[8,2,32,1024]{3,2,1,0:T(8,128)}), f32[16,2,32,1024]{3,2,1,0:T(8,128)}) %all-gather.13.cloned.1.call-update) | async-done | bytes 4194320 | tf_op jit(solution)/shard_map/all_gather | solution.py:31
  80.0 2.7 copy.13
  82.7 0.8 copy-done.1
  83.5 0.7 copy-done.4
  84.2 8.1 %multiply_reduce_fusion.1 = f32[1024]{0:T(1024)S(1)} fusion(f32[1024,1024]{0,1:T(8,128)S(1)} %copy-done.1, f32[1024]{0:T(1024)S(1)} %copy-done.8, f32[1024]{0:T(1024)S(1)} %copy-done.9, bf16[1024,1024]{1,0:T(8,128)(2,1)S(1)} %bitcast.37, f32[1024,1024]{1,0:T(8,128)S(1)} %bitcast.36), kind=kOutput, calls=%fused_computation.8 | convolution fusion | flops 12889095168 | bytes 10498048 | tf_op jit(solution)/shard_map/it,ih->th/dot_general | solution.py:79
  92.3 9.6 %all_to_all.30 = f32[8,1,1024]{2,1,0:T(1,128)S(1)} all-to-all(f32[8,1,1024]{2,1,0:T(1,128)S(1)} %broadcast_in_dim.10), channel_id=1, replica_groups=mesh['grp_0'=2,'grp_1'=4,'smp_0'=2,'smp_1'=8,'smp_2'=2] {'grp_0','grp_1'}, dimensions={0} | all-to-all | bytes 65536 | tf_op jit(solution)/shard_map/all_to_all | solution.py:44
  101.9 0.7 fusion.11
  102.5 0.7 broadcast_in_dim.11
  103.2 20.1 %all_to_all.31 = f32[32,1,1]{2,1,0:T(1,128)S(1)} all-to-all(f32[32,1,1]{2,1,0:T(1,128)S(1)} %broadcast_in_dim.11), channel_id=1, replica_groups=mesh['grp_0'=2,'grp_1'=4,'smp_0'=2,'smp_1'=8,'smp_2'=2] {'smp_0','smp_1'..., dimensions={0} | all-to-all | bytes 256 | tf_op jit(solution)/shard_map/all_to_all | solution.py:44
  123.3 0.6 reduce_sum.166
  124.6 0.6 multiply_reduce_fusion.8
  125.2 11.3 %fusion.4 = f32[1024,1024]{1,0:T(8,128)} fusion(bf16[1024,1024]{1,0:T(8,128)(2,1)} %copy-done.6, f32[1024,1024]{0,1:T(8,128)} %fusion.12, f32[1024]{0:T(1024)S(1)} %get-tuple-element.21, f32[1024]{0:T(1024)S(1)} %copy-done.9), kind=kOutput, calls=%fused_computation.6 | convolution fusion | flops 12886999040 | bytes 10493952 | tf_op jit(solution)/shard_map/it,th->ih/dot_general | solution.py:100
  136.5 5.9 %fusion.6 = f32[1,1024]{1,0:T(1,128)S(1)} fusion(f32[1024,1]{0,1:T(1,128)S(1)} %bitcast.44, f32[1024,1024]{0,1:T(8,128)} %fusion.12, f32[1024]{0:T(1024)S(1)} %copy-done.9), kind=kOutput, calls=%fused_computation.11 | convolution fusion | flops 13631488 | bytes 4206592 | tf_op jit(solution)/shard_map/dot_general | solution.py:113
  142.5 0.7 broadcast_in_dim.12
  143.2 4.3 all-to-all-start.2
  147.5 0.0 all-gather.15.cloned.1.call-start
  147.6 0.7 multiply_reduce_fusion.9
  149.0 0.7 multiply_reduce_fusion.4
  151.0 4.6 all-reduce.4
  155.7 7.6 %all-reduce.1 = (f32[]{:T(128)}, f32[]{:T(128)}) all-reduce(f32[]{:T(128)} %get-tuple-element.14, f32[]{:T(128)} %get-tuple-element.15), channel_id=1, replica_groups=mesh['grp_0'=2,'grp_1'=4,'smp_0'=2,'smp_1'=8,'smp_2'=2] {'grp_1'}, use_global_device_ids=true, to_apply=%region_3.0 | all-reduce | flops 2 | bytes 16 | tf_op jit(solution)/shard_map/psum | solution.py:19
  163.3 5.9 %all-reduce.3 = (f32[]{:T(128)}, f32[]{:T(128)}) all-reduce(f32[]{:T(128)} %get-tuple-element.8, f32[]{:T(128)} %get-tuple-element.9), channel_id=1, replica_groups=mesh['grp_0'=2,'grp_1'=4,'smp_0'=2,'smp_1'=8,'smp_2'=2] {'smp_0'}, use_global_device_ids=true, to_apply=%region_4.0 | all-reduce | flops 2 | bytes 16 | tf_op jit(solution)/shard_map/psum | solution.py:19
  169.2 14.0 %all-reduce = (f32[]{:T(128)}, f32[]{:T(128)}) all-reduce(f32[]{:T(128)} %get-tuple-element.12, f32[]{:T(128)} %get-tuple-element.13), channel_id=1, replica_groups=mesh['grp_0'=2,'grp_1'=4,'smp_0'=2,'smp_1'=8,'smp_2'=2] {'smp_1'}, use_global_device_ids=true, to_apply=%region_5.0 | all-reduce | flops 2 | bytes 16 | tf_op jit(solution)/shard_map/psum | solution.py:19
  183.2 10.8 %all-reduce.2 = (f32[]{:T(128)}, f32[]{:T(128)}) all-reduce(f32[]{:T(128)} %get-tuple-element.6, f32[]{:T(128)} %get-tuple-element.7), channel_id=1, replica_groups=mesh['grp_0'=2,'grp_1'=4,'smp_0'=2,'smp_1'=8,'smp_2'=2] {'smp_2'}, use_global_device_ids=true, to_apply=%region_6.0 | all-reduce | flops 2 | bytes 16 | tf_op jit(solution)/shard_map/psum | solution.py:19
  195.4 0.1 reduce_sum.169
  195.5 0.6 multiply_reduce_fusion.7
  196.7 55.0 %reduce-scatter.2.cloned.1.call-done = f32[32,1024]{1,0:T(8,128)} async-done(((f32[1024,1024]{1,0:T(8,128)}), f32[32,1024]{1,0:T(8,128)}) %reduce-scatter.2.cloned.1.call-update) | async-done | bytes 131088 | tf_op jit(solution)/shard_map/reduce_scatter | solution.py:99
  251.7 1.5 multiply_reduce_fusion.3
  253.9 4.3 psum.150
  258.2 9.1 %psum.151 = f32[]{:T(128)} all-reduce(f32[]{:T(128)} %psum.150), channel_id=1, replica_groups=mesh['grp_0'=2,'grp_1'=4,'smp_0'=2,'smp_1'=8,'smp_2'=2] {'grp_1'}, use_global_device_ids=true, to_apply=%region_22.0 | all-reduce | flops 1 | bytes 8 | tf_op jit(solution)/shard_map/psum | solution.py:19
  267.3 5.9 %psum.152 = f32[]{:T(128)} all-reduce(f32[]{:T(128)} %psum.151), channel_id=1, replica_groups=mesh['grp_0'=2,'grp_1'=4,'smp_0'=2,'smp_1'=8,'smp_2'=2] {'smp_0'}, use_global_device_ids=true, to_apply=%region_23.0 | all-reduce | flops 1 | bytes 8 | tf_op jit(solution)/shard_map/psum | solution.py:19
  273.2 13.3 %psum.153 = f32[]{:T(128)} all-reduce(f32[]{:T(128)} %psum.152), channel_id=1, replica_groups=mesh['grp_0'=2,'grp_1'=4,'smp_0'=2,'smp_1'=8,'smp_2'=2] {'smp_1'}, use_global_device_ids=true, to_apply=%region_24.0 | all-reduce | flops 1 | bytes 8 | tf_op jit(solution)/shard_map/psum | solution.py:19
  286.5 16.3 %psum.154 = f32[]{:T(128)} all-reduce(f32[]{:T(128)} %psum.153), channel_id=1, replica_groups=mesh['grp_0'=2,'grp_1'=4,'smp_0'=2,'smp_1'=8,'smp_2'=2] {'smp_2'}, use_global_device_ids=true, to_apply=%region_25.0 | all-reduce | flops 1 | bytes 8 | tf_op jit(solution)/shard_map/psum | solution.py:19
  304.1 1.6 multiply_reduce_fusion.2
  305.6 7.0 %all-gather.3 = f32[64,1024]{1,0:T(8,128)} all-gather(f32[32,1024]{1,0:T(8,128)S(1)} %get-tuple-element.19), channel_id=5, replica_groups=mesh['grp_0'=2,'grp_1'=4,'smp_0'=2,'smp_1'=8,'smp_2'=2] {'smp_0'}, dimensions={0}, use_global_device_ids=true | all-gather | bytes 393216 | tf_op jit(solution)/shard_map/all_gather | solution.py:31
  312.6 0.3 all-gather.17.cloned.1.call-start
  312.9 33.0 %all-gather.15.cloned.1.call-done = f32[16,32,1024]{2,1,0:T(8,128)} async-done(((f32[2,32,1024]{2,1,0:T(8,128)}), f32[16,32,1024]{2,1,0:T(8,128)}) %all-gather.15.cloned.1.call-update) | async-done | bytes 2097168 | tf_op jit(solution)/shard_map/all_gather | solution.py:31
  345.9 0.7 multiply_reduce_fusion.5
  346.6 23.5 %all-gather.17.cloned.1.call-done = f32[16,2,32,1024]{3,2,1,0:T(8,128)} async-done(((f32[8,2,32,1024]{3,2,1,0:T(8,128)}), f32[16,2,32,1024]{3,2,1,0:T(8,128)}) %all-gather.17.cloned.1.call-update) | async-done | bytes 4194320 | tf_op jit(solution)/shard_map/all_gather | solution.py:31
  370.0 2.7 copy.18
  372.7 0.8 copy-done.2
  373.5 0.7 copy-done.5
  374.2 8.1 %multiply_reduce_fusion = f32[1024]{0:T(1024)S(1)} fusion(f32[1024,1024]{0,1:T(8,128)S(1)} %copy-done.2, f32[1024]{0:T(1024)S(1)} %get-tuple-element.17, f32[1024]{0:T(1024)S(1)} %copy-done.9, bf16[1024,1024]{1,0:T(8,128)(2,1)S(1)} %bitcast.38, f32[1024,1024]{1,0:T(8,128)S(1)} %bitcast.35), kind=kOutput, calls=%fused_computation.5 | convolution fusion | flops 12889095168 | bytes 10498048 | tf_op jit(solution)/shard_map/it,ih->th/dot_general | solution.py:79
  382.3 9.6 %all_to_all.32 = f32[8,1,1024]{2,1,0:T(1,128)S(1)} all-to-all(f32[8,1,1024]{2,1,0:T(1,128)S(1)} %broadcast_in_dim.13), channel_id=1, replica_groups=mesh['grp_0'=2,'grp_1'=4,'smp_0'=2,'smp_1'=8,'smp_2'=2] {'grp_0','grp_1'}, dimensions={0} | all-to-all | bytes 65536 | tf_op jit(solution)/shard_map/all_to_all | solution.py:44
  391.9 0.7 fusion.10
  392.6 1.3 broadcast_in_dim.14
  393.9 10.9 %all-to-all-start.4 = ((f32[32,1,1]{2,1,0:T(1,128)}), f32[32,1,1]{2,1,0:T(1,128)S(1)}, u32[]{:S(2)}, u32[]{:S(2)}) async-start(f32[32,1,1]{2,1,0:T(1,128)} %broadcast_in_dim.14), calls=%async_computation.5 | async-start | bytes 32768 | tf_op jit(solution)/shard_map/all_to_all | solution.py:44
  406.2 8.0 %all-to-all-done.4 = f32[32,1,1]{2,1,0:T(1,128)S(1)} async-done(((f32[32,1,1]{2,1,0:T(1,128)}), f32[32,1,1]{2,1,0:T(1,128)S(1)}, u32[]{:S(2)}, u32[]{:S(2)}) %all-to-all-start.4) | async-done | bytes 160 | tf_op jit(solution)/shard_map/all_to_all | solution.py:44
  414.1 0.6 reduce_sum.174
  415.4 0.6 multiply_reduce_fusion.6
  416.7 4.3 psum.155
  421.0 7.5 %psum.156 = f32[]{:T(128)} all-reduce(f32[]{:T(128)} %psum.155), channel_id=1, replica_groups=mesh['grp_0'=2,'grp_1'=4,'smp_0'=2,'smp_1'=8,'smp_2'=2] {'grp_1'}, use_global_device_ids=true, to_apply=%region_34.0 | all-reduce | flops 1 | bytes 8 | tf_op jit(solution)/shard_map/psum | solution.py:19
  428.5 5.9 %psum.157 = f32[]{:T(128)} all-reduce(f32[]{:T(128)} %psum.156), channel_id=1, replica_groups=mesh['grp_0'=2,'grp_1'=4,'smp_0'=2,'smp_1'=8,'smp_2'=2] {'smp_0'}, use_global_device_ids=true, to_apply=%region_35.0 | all-reduce | flops 1 | bytes 8 | tf_op jit(solution)/shard_map/psum | solution.py:19
  434.3 11.7 %psum.158 = f32[]{:T(128)} all-reduce(f32[]{:T(128)} %psum.157), channel_id=1, replica_groups=mesh['grp_0'=2,'grp_1'=4,'smp_0'=2,'smp_1'=8,'smp_2'=2] {'smp_1'}, use_global_device_ids=true, to_apply=%region_36.0 | all-reduce | flops 1 | bytes 8 | tf_op jit(solution)/shard_map/psum | solution.py:19
  446.0 11.6 %psum.159 = f32[]{:T(128)} all-reduce(f32[]{:T(128)} %psum.158), channel_id=1, replica_groups=mesh['grp_0'=2,'grp_1'=4,'smp_0'=2,'smp_1'=8,'smp_2'=2] {'smp_2'}, use_global_device_ids=true, to_apply=%region_37.0 | all-reduce | flops 1 | bytes 8 | tf_op jit(solution)/shard_map/psum | solution.py:19
  458.9 0.6 multiply_add_fusion.2
  459.5 0.7 multiply_add_fusion
  (26 shorter events, 0.2 us)
Async XLA Ops:
  7.2 52.8 %copy-start = (bf16[1024,1024]{1,0:T(8,128)(2,1)S(1)}, bf16[1024,1024]{1,0:T(8,128)(2,1)}, u32[]{:S(2)}) copy-start(bf16[1024,1024]{1,0:T(8,128)(2,1)} %param.6) | copy-start | bytes 6291460
  7.2 50.4 %copy-start.7 = (s32[32,1024]{1,0:T(8,128)S(1)}, s32[32,1024]{1,0:T(8,128)}, u32[]{:S(2)}) copy-start(s32[32,1024]{1,0:T(8,128)} %param.5) | copy-start | bytes 393220
  7.2 48.5 %all-gather.11.cloned.1.call-start = ((), (), s32[]{:S(2)}) async-start(), calls=%async_computation.7 | async-start | bytes 2359296 | tf_op jit(solution)/shard_map/all_gather | solution.py:31
  15.8 64.2 %all-gather.13.cloned.1.call-start = ((), (), s32[]{:S(2)}) async-start(), calls=%async_computation.8 | async-start | bytes 6291456 | tf_op jit(solution)/shard_map/all_gather | solution.py:31
  55.8 196.0 %reduce-scatter.2.cloned.1.call-start = ((), (), s32[]{:S(2)}) async-start(), calls=%async_computation.6 | async-start | bytes 4325376 | tf_op jit(solution)/shard_map/reduce_scatter | solution.py:99
  57.6 2.4 copy-start.6
  80.0 3.4 copy-start.1
  80.0 4.1 copy-start.4
  80.0 4.1 copy-start.8
  80.0 4.1 copy-start.9
  136.5 12.5 %copy-start.3 = (f32[32,1024]{1,0:T(8,128)S(1)}, f32[32,1024]{1,0:T(8,128)}, u32[]{:S(2)}) copy-start(f32[32,1024]{1,0:T(8,128)} %param.8) | copy-start | bytes 393220
  143.2 52.1 %all-to-all-start.2 = ((f32[32,1,1024]{2,1,0:T(1,128)}), f32[32,1,1024]{2,1,0:T(1,128)S(1)}, u32[]{:S(2)}, u32[]{:S(2)}) async-start(f32[32,1,1024]{2,1,0:T(1,128)} %broadcast_in_dim.12), calls=%async_computation.3 | async-start | bytes 262144 | tf_op jit(solution)/shard_map/all_to_all | solution.py:44
  147.5 198.4 %all-gather.15.cloned.1.call-start = ((), (), s32[]{:S(2)}) async-start(), calls=%async_computation.9 | async-start | bytes 2359296 | tf_op jit(solution)/shard_map/all_gather | solution.py:31
  312.6 57.4 %all-gather.17.cloned.1.call-start = ((), (), s32[]{:S(2)}) async-start(), calls=%async_computation.10 | async-start | bytes 6291456 | tf_op jit(solution)/shard_map/all_gather | solution.py:31
  370.0 3.4 copy-start.2
  370.0 4.1 copy-start.5
  393.9 20.2 %all-to-all-start.4 = ((f32[32,1,1]{2,1,0:T(1,128)}), f32[32,1,1]{2,1,0:T(1,128)S(1)}, u32[]{:S(2)}, u32[]{:S(2)}) async-start(f32[32,1,1]{2,1,0:T(1,128)} %broadcast_in_dim.14), calls=%async_computation.5 | async-start | bytes 32768 | tf_op jit(solution)/shard_map/all_to_all | solution.py:44
Sparse Core Ops, SparseCore 0:
  16.0 39.7 all-gather.10
  57.5 22.4 all-gather.12
  136.6 115.0 reduce-scatter.1
  312.8 33.0 all-gather.14
  347.5 22.4 all-gather.16
where the time goes:
time: 468 us; the launch traced here: 467 us
  blocking collectives  187 us (40%)
  waiting for transfers between devices  175 us (37%)
  matrix products  37.8 us (8%)
  between operations  24.5 us (5%)
  starting transfers between devices  15.7 us (3%)
  other arithmetic  15.1 us (3%)
  local copies, waits for them, and re-layouts  11.1 us (2%)
    psum x15, blocking collectives, one_axis_at_a_time(): return functools.reduce(lax.psum, axes, value)  133 us
    all_gather x4, waiting for transfers between devices, all_blocks(): tiles = lax.all_gather(tiles, axes[k])  112 us
    reduce_scatter x1, waiting for transfers between devices, body(): lax.psum_scatter(jnp.einsum('it,th->ih', spins, weighted, precision=lax.P...  55 us
    all_to_all x3, blocking collectives, sent_to_all(): lax.all_to_all(jnp.broadcast_to(value[None], (size, *value.shape)), axis,...  39.2 us
    dot_general x2, matrix products, body(): jnp.einsum('it,ih->th', spins, gather_axes(direction_w, SMP, (0, 1, 2), 0...  16.2 us
    all_gather x2, blocking collectives, all_blocks(): tiles = lax.all_gather(tiles, axes[k])  15.5 us
    all_to_all x2, starting transfers between devices, sent_to_all(): lax.all_to_all(jnp.broadcast_to(value[None], (size, *value.shape)), axis,...  15.3 us
    dot_general x1, matrix products, body(): jnp.einsum('it,th->ih', spins, weighted, precision=lax.Precision.HIGHEST,...  11.3 us
  transfers between devices with their start and end apart: 7, of which 6 were waited for; matrix products, arithmetic and copies ran while one was open for 4% of the time, Pallas kernels for 0%

commit v1 on v0

v1 whole, which is shorter than its diff:
```python
import functools

import jax
import jax.numpy as jnp
from jax import lax
from jax.experimental import pallas as pl
from jax.experimental.pallas import tpu as pltpu
from jax.sharding import PartitionSpec as P

MESH = pl.DeviceIdType.MESH
LAMBDA = 0.01
F32 = jnp.float32
BF16 = jnp.bfloat16
LANES = 128


def split(x):
    hi = x.astype(BF16)
    return hi, (x - hi.astype(F32)).astype(BF16)


def folded(x):
    rows, cols = x.shape
    tiles = [x[r : r + 8, k : k + LANES] for r in range(0, rows, 8) for k in range(0, cols, LANES)]
    return functools.reduce(lambda a, b: a + b, tiles)


def total(x):
    return jnp.sum(jnp.sum(x, axis=0, keepdims=True), axis=1, keepdims=True)


def kernel(ng, nz, count, spk, w_hbm, hb, fw, fb, out_w, out_b,
           pk, wv, wt, fc, ft, sgn, hid, ch, acc, vbuf, v1, s2, r2, s3, r3, x1s, x1, x2s, x2,
           w1, s4, r4, s5, r5, gb, rs_s, rs_r, gall, gown, cols,
           local_sem, send, pk_sem, fa_sem, fx_sem, v1_sem, v2_sem, v3_sem, x1_sem, x2_sem, w1_sem, w2_sem, w3_sem,
           rs_sem, ag_sem, gz_sem):
    ns = 4 * nz
    rows = 8 * ns
    tok = spk.shape[1]
    tiles = tok // LANES
    s = lax.axis_index("smp")
    g = lax.axis_index("grp")
    xh = s // (2 * nz)
    z = (s // 2) % nz
    c = s % 2
    q_me = 2 * xh + c
    q_core = 2 * xh + 1 - c
    q_x = 2 * (1 - xh) + c
    q_far = 2 * (1 - xh) + 1 - c
    core = s + 1 - 2 * c
    across = s + (2 * nz) * (1 - 2 * xh)

    def z_index(k):
        return 2 * nz * xh + 2 * k + c

    def remote(src, dst, ssem, rsem, dev):
        return pltpu.make_async_remote_copy(src_ref=src, dst_ref=dst, send_sem=ssem, recv_sem=rsem,
                                            device_id=dev, device_id_type=MESH)

    def peers(n, me, act):
        def step(j, carry):
            act(lax.rem(me + j, n))
            return carry
        lax.fori_loop(1, n, step, 0)

    class Exchange:
        def __init__(self, n, me, dev, src, dst, number, sems):
            self.n, self.me, self.dev, self.src, self.dst = n, me, dev, src, dst
            self.ssem, self.sems = send.at[number], sems

        def copy(self, peer, slot):
            return remote(self.src(peer), self.dst(slot), self.ssem, self.sems.at[slot], self.dev(peer))

        def start(self):
            peers(self.n, self.me, lambda p: self.copy(p, self.me).start())

        def wait_from(self, p):
            self.copy(p, p).wait_recv()

        def wait(self):
            peers(self.n, self.me, self.wait_from)

        def drain(self):
            peers(self.n, self.me, lambda p: self.copy(p, self.me).wait_send())

    def over_z(src, dst, number, sems):
        return Exchange(nz, z, lambda p: {"smp": z_index(p)}, src, dst, number, sems)

    def over_grp(src, dst, number, sems):
        return Exchange(ng, g, lambda p: {"grp": p}, src, dst, number, sems)

    def over_smp(src, dst, number, sems):
        return Exchange(ns, s, lambda p: {"smp": p}, src, dst, number, sems)

    def lane(k, width=LANES):
        return pl.ds(pl.multiple_of(k * width, width), width)

    def block(k, height=32):
        return pl.ds(pl.multiple_of(k * height, height), height)

    w_copy = pltpu.make_async_copy(w_hbm.at[:, lane(z)], wv, local_sem.at[0])
    w_copy.start()

    barrier = pltpu.get_barrier_semaphore()
    peers(ns, s, lambda p: pl.semaphore_signal(barrier, inc=1, device_id={"smp": p}, device_id_type=MESH))
    peers(ng, g, lambda p: pl.semaphore_signal(barrier, inc=1, device_id={"grp": p}, device_id_type=MESH))

    ex_pk = over_z(lambda p: spk, lambda k: pk.at[k], 0, pk_sem)
    ex_fa = over_z(lambda p: fw.at[:, lane(p)], lambda k: fc.at[q_me, block(k)], 1, fa_sem)
    ex_v1 = over_z(lambda p: vbuf.at[p], lambda k: v1.at[k], 2, v1_sem)
    ex_v2 = over_grp(lambda p: s2, lambda k: r2.at[k], 3, v2_sem)
    ex_v3 = over_smp(lambda p: s3, lambda k: r3.at[k], 4, v3_sem)
    ex_x1 = over_smp(lambda p: x1s, lambda k: x1.at[k], 5, x1_sem)
    ex_x2 = over_smp(lambda p: x2s, lambda k: x2.at[k], 6, x2_sem)
    ex_w1 = over_z(lambda p: vbuf.at[nz + p], lambda k: w1.at[k], 7, w1_sem)
    ex_w2 = over_grp(lambda p: s4, lambda k: r4.at[k], 8, w2_sem)
    ex_w3 = over_smp(lambda p: s5, lambda k: r5.at[k], 9, w3_sem)
    ex_gz = over_z(lambda p: gall.at[q_me, block(p)], lambda k: gown.at[:, lane(k)], 10, gz_sem)

    def gather(buf, first, sems):
        to_core = remote(buf.at[q_me], buf.at[q_me], send.at[first], sems.at[0], {"smp": core})
        to_x = remote(buf.at[q_me], buf.at[q_me], send.at[first + 1], sems.at[1], {"smp": across})
        on = remote(buf.at[q_x], buf.at[q_x], send.at[first + 2], sems.at[2], {"smp": core})
        from_core = remote(buf.at[q_core], buf.at[q_core], send.at[first], sems.at[0], {"smp": core})
        from_x = remote(buf.at[q_x], buf.at[q_x], send.at[first + 1], sems.at[1], {"smp": across})
        from_on = remote(buf.at[q_far], buf.at[q_far], send.at[first + 2], sems.at[2], {"smp": core})
        return to_core, to_x, on, from_core, from_x, from_on

    fx = gather(fc, 11, fx_sem)
    ag = gather(gall, 14, ag_sem)

    bit = jnp.left_shift(jnp.int32(1), lax.broadcasted_iota(jnp.int32, (32, tok), 0))

    def unpack(words, j):
        for xq in range(2):
            for cq in range(2):
                for k in range(nz):
                    row = words[pl.ds(2 * nz * xq + 2 * k + cq, 1), :]
                    up = jnp.where(jnp.bitwise_and(jnp.broadcast_to(row, (32, tok)), bit) != 0, F32(1), F32(-1))
                    at = ((2 * xq + cq) * nz + k) * 32
                    sgn[pl.ds(at, 32), lane(j, tok)] = up.astype(BF16)

    def hidden(j):
        pre = jnp.dot(wt[...], sgn[:, lane(j, tok)], preferred_element_type=F32)
        for r in range(tiles):
            part = pre[:, r * LANES : (r + 1) * LANES] + cols[0]
            hid[:, lane(j * tiles + r)] = jnp.tanh(part)

    cols[0] = jnp.broadcast_to(hb[pl.ds(z, 1), :], (LANES, LANES)).T
    cols[1] = jnp.broadcast_to(fb[pl.ds(z, 1), :], (LANES, LANES)).T
    unpack(spk, 0)
    w_copy.wait()
    for q in range(4):
        parts = [wv[pl.ds(32 * (2 * nz * (q // 2) + 2 * k + q % 2), 32), :] for k in range(nz)]
        wt[:, q * 32 * nz : (q + 1) * 32 * nz] = jnp.concatenate(parts, axis=0).astype(F32).T.astype(BF16)

    pl.semaphore_wait(barrier, ns - 1 + ng - 1)
    ex_fa.start()
    ex_pk.start()
    fc[q_me, block(z), :] = fw[:, lane(z)]
    hidden(0)
    ex_fa.wait()
    fx[0].start()
    fx[1].start()

    def shard(j):
        d = (j + 1) // 2
        return lax.rem(z + (2 * (j % 2) - 1) * d + nz, nz)

    def arrive(j, carry):
        k = shard(j)
        ex_pk.wait_from(k)
        unpack(pk.at[k], j)
        hidden(j)
        return carry

    half = (nz + 1) // 2
    lax.fori_loop(1, half, arrive, 0)
    fx[4].wait_recv()
    fx[2].start()
    lax.fori_loop(half, nz, arrive, 0)
    fx[3].wait_recv()
    fx[5].wait_recv()

    def transposed(buf, q):
        hi, lo = split(buf[q].T)
        at = q * 32 * nz
        ft[:LANES, at : at + 32 * nz] = hi
        ft[LANES:, at : at + 32 * nz] = lo

    def values(base, col):
        def step(j, carry):
            k = shard(j)
            res = jnp.dot(ft[...], sgn[:, lane(j, tok)], preferred_element_type=F32)
            for r in range(tiles):
                both = res[:LANES, r * LANES : (r + 1) * LANES] + res[LANES:, r * LANES : (r + 1) * LANES]
                prod = (both + cols[col]) * hid[:, lane(j * tiles + r)]
                vbuf[base + k, pl.ds(r, 1), :] = jnp.sum(prod, axis=0, keepdims=True)
            return carry
        lax.fori_loop(0, nz, step, 0)

    for q in range(4):
        transposed(fc, q)
    values(0, 1)

    ex_v1.start()
    v1[z] = vbuf[z]
    s2[1] = folded(fw[...] * fw[...]) + folded(fb[...] * fb[...]) * F32(1.0 / ns)
    ex_v1.wait()
    s2[0] = functools.reduce(lambda a, b: a + b, [v1[k] for k in range(nz)])
    ex_v2.start()
    r2[g] = s2[...]
    ex_v2.wait()
    s3[...] = functools.reduce(lambda a, b: a + b, [r2[k] for k in range(ng)])
    ex_v3.start()
    r3[s] = s3[...]
    ex_v3.wait()
    sums = functools.reduce(lambda a, b: a + b, [r3[k] for k in range(ns)])
    mean = total(sums[0]) * F32(1.0 / count)
    norm0 = total(sums[1])
    square = jnp.zeros((8, LANES), F32)
    for k in range(ns):
        off = r3[k, 0] - mean
        square += off * off
    curvature = total(square) * F32(1.0 / count) + F32(LAMBDA) * norm0
    alpha0 = norm0 / curvature

    def weigh(j, carry):
        own = r3[z_index(shard(j)), 0] - mean
        bias = carry
        for r in range(tiles):
            prod = hid[:, lane(j * tiles + r)] * own[r : r + 1, :]
            hi, lo = split(prod)
            ch[:LANES, lane(j * tiles + r)] = hi
            ch[LANES:, lane(j * tiles + r)] = lo
            bias = bias + prod
        return bias

    gb[...] = jnp.zeros((LANES, LANES), F32)

    def weigh_step(j, carry):
        gb[...] = weigh(j, gb[...])
        return carry

    lax.fori_loop(0, nz, weigh_step, 0)
    x1s[...] = jnp.broadcast_to(jnp.sum(gb[...].T, axis=0, keepdims=True), (8, LANES))
    ex_x1.start()
    x1[s] = x1s[...]

    height = 32 * nz

    def image(q):
        res = lax.dot_general(sgn[block(q, height), :], ch[...], (((1,), (1,)), ((), ())), preferred_element_type=F32)
        return res[:, :LANES] + res[:, LANES:]

    hop0 = remote(rs_s.at[0], rs_r.at[0], send.at[17], rs_sem.at[0], {"smp": core})
    hop1 = remote(rs_s.at[1], rs_r.at[1], send.at[18], rs_sem.at[1], {"smp": across})
    hop2 = remote(rs_s.at[2], rs_r.at[2], send.at[19], rs_sem.at[2], {"smp": core})
    rs_s[0] = image(q_far)
    hop0.start()
    part = image(q_x)
    hop0.wait_recv()
    rs_s[1] = part + rs_r[0]
    hop1.start()
    rs_s[2] = image(q_core)
    hop2.start()
    acc[...] = image(q_me)
    hop2.wait_recv()
    acc[...] = acc[...] + rs_r[2]
    hop1.wait_recv()
    gall[q_me] = acc[...] + rs_r[1]
    ag[0].start()
    ag[1].start()
    ex_gz.start()
    gown[:, lane(z)] = gall[q_me, block(z), :]

    ex_x1.wait()
    for k in range(nz):
        at = [x1[2 * nz * xq + 2 * k + cq, 0:1, :] for xq in range(2) for cq in range(2)]
        gb[pl.ds(k, 1), :] = (at[0] + at[1]) + (at[2] + at[3])
    if nz < 8:
        gb[nz:8, :] = jnp.zeros((8 - nz, LANES), F32)
    image_b = gb[:8, :]
    cols[2] = jnp.broadcast_to(gb[pl.ds(z, 1), :], (LANES, LANES)).T
    inv = F32(1.0 / count)
    res_b = fb[...] - alpha0 * (image_b * inv + F32(LAMBDA) * fb[...])
    own_f = fc[q_me]
    res_w = own_f - alpha0 * (gall[q_me] * inv + F32(LAMBDA) * own_f)
    x2s[0] = folded(res_w * res_w) + res_b * res_b * F32(1.0 / ns)
    x2s[1] = folded(res_w * own_f) + res_b * fb[...] * F32(1.0 / ns)
    ex_x2.start()
    x2[s] = x2s[...]
    ag[4].wait_recv()
    ag[2].start()
    ag[3].wait_recv()
    ag[5].wait_recv()
    for q in range(4):
        transposed(gall, q)
    values(nz, 2)

    ex_w1.start()
    w1[z] = vbuf[nz + z]
    ex_x2.wait()
    s4[1:3] = functools.reduce(lambda a, b: a + b, [x2[k] for k in range(ns)])
    ex_w1.wait()
    s4[0] = functools.reduce(lambda a, b: a + b, [w1[k] for k in range(nz)])
    ex_w2.start()
    r4[g] = s4[...]
    ex_w2.wait()
    sums = functools.reduce(lambda a, b: a + b, [r4[k] for k in range(ng)])
    norm1 = total(sums[1])
    cross = total(sums[2])
    beta = norm1 / norm0
    scale_f = F32(1.0) - alpha0 * F32(LAMBDA) + beta
    s5[...] = scale_f * (r3[s, 0] - mean) - (alpha0 * inv) * sums[0]
    ex_w3.start()
    r5[s] = s5[...]
    ex_w3.wait()
    mean1 = total(functools.reduce(lambda a, b: a + b, [r5[k] for k in range(ns)])) * inv
    square = jnp.zeros((8, LANES), F32)
    for k in range(ns):
        off = r5[k] - mean1
        square += off * off
    norm_d = norm1 + F32(2.0) * beta * cross + beta * beta * norm0
    curvature = total(square) * inv + F32(LAMBDA) * norm_d
    alpha1 = norm1 / curvature
    factor_f = alpha0 + alpha1 * scale_f
    factor_g = alpha1 * alpha0 * inv
    ex_gz.wait()
    out_w[...] = factor_f * fw[...] - factor_g * gown[...]
    out_b[...] = factor_f * fb[...] - factor_g * image_b

    for ex in (ex_pk, ex_fa, ex_v1, ex_v2, ex_v3, ex_x1, ex_x2, ex_w1, ex_w2, ex_w3, ex_gz):
        ex.drain()
    for move in (*fx[:3], *ag[:3], hop0, hop1, hop2):
        move.wait_send()


def call(ng, nz, count, spk, w, hb, fw, fb):
    ns = 4 * nz
    tok = spk.shape[1]
    words, height = spk.shape[0], 32 * nz
    nv = 32 * words
    tile = (8, LANES)
    dma = pltpu.SemaphoreType.DMA
    vmem = pl.BlockSpec(memory_space=pltpu.VMEM)
    scratch = [
        pltpu.VMEM((nz, words, tok), jnp.int32),
        pltpu.VMEM((nv, LANES), BF16),
        pltpu.VMEM((LANES, nv), BF16),
        pltpu.VMEM((4, height, LANES), F32),
        pltpu.VMEM((2 * LANES, nv), BF16),
        pltpu.VMEM((nv, nz * tok), BF16),
        pltpu.VMEM((LANES, nz * tok), F32),
        pltpu.VMEM((2 * LANES, nz * tok), BF16),
        pltpu.VMEM((height, LANES), F32),
        pltpu.VMEM((2 * nz, *tile), F32),
        pltpu.VMEM((nz, *tile), F32),
        pltpu.VMEM((2, *tile), F32),
        pltpu.VMEM((ng, 2, *tile), F32),
        pltpu.VMEM((2, *tile), F32),
        pltpu.VMEM((ns, 2, *tile), F32),
        pltpu.VMEM(tile, F32),
        pltpu.VMEM((ns, *tile), F32),
        pltpu.VMEM((2, *tile), F32),
        pltpu.VMEM((ns, 2, *tile), F32),
        pltpu.VMEM((nz, *tile), F32),
        pltpu.VMEM((3, *tile), F32),
        pltpu.VMEM((ng, 3, *tile), F32),
        pltpu.VMEM(tile, F32),
        pltpu.VMEM((ns, *tile), F32),
        pltpu.VMEM((LANES, LANES), F32),
        pltpu.VMEM((3, height, LANES), F32),
        pltpu.VMEM((3, height, LANES), F32),
        pltpu.VMEM((4, height, LANES), F32),
        pltpu.VMEM((32, nz * LANES), F32),
        pltpu.VMEM((3, LANES, LANES), F32),
        dma((1,)),
        dma((20,)),
        dma((nz,)),
        dma((nz,)),
        dma((3,)),
        dma((nz,)),
        dma((ng,)),
        dma((ns,)),
        dma((ns,)),
        dma((ns,)),
        dma((nz,)),
        dma((ng,)),
        dma((ns,)),
        dma((3,)),
        dma((3,)),
        dma((nz,)),
    ]
    return pl.pallas_call(
        functools.partial(kernel, ng, nz, count),
        out_shape=(jax.ShapeDtypeStruct(fw.shape, F32), jax.ShapeDtypeStruct(tile, F32)),
        in_specs=[vmem, pl.BlockSpec(memory_space=pl.ANY), vmem, vmem, vmem],
        out_specs=(vmem, vmem),
        scratch_shapes=scratch,
        compiler_params=pltpu.CompilerParams(collective_id=0, has_side_effects=True,
                                             vmem_limit_bytes=60 * 1024 * 1024),
        name="step",
    )(spk, w, hb, fw, fb)


def solution(mesh):
    ng, ns = mesh.shape["grp"], mesh.shape["smp"]
    nz = ns // 4

    def body(spk, w, hb, fw, fb):
        count = spk.shape[1] * ns
        tile = (8, LANES)
        pad = 8 * LANES - hb.shape[0]
        hb, fb = (jnp.pad(v, (0, pad)).reshape(tile) for v in (hb, fb))
        out_w, out_b = call(ng, nz, count, spk, w, hb, fw, fb)
        return out_w, out_b.reshape(-1)[: nz * LANES]

    return jax.shard_map(body, mesh=mesh,
                         in_specs=(P(None, "smp"), P(None, "grp"), P("grp"), P("smp", "grp"), P("grp")),
                         out_specs=(P("smp", "grp"), P("grp")), check_vma=False)
```

time: 468 us -> 116 us (0.25)
  blocking collectives: 187 us -> 0 us
  waiting for transfers between devices: 175 us -> 0 us
  Pallas kernels: 0 us -> 113 us
  matrix products: 37.8 us -> 0 us
  between operations: 24.5 us -> 0.64 us
  starting transfers between devices: 15.7 us -> 0 us
  other arithmetic: 15.1 us -> 0 us
  local copies, waits for them, and re-layouts: 11.1 us -> 2.85 us
    psum x15 -> x0, blocking collectives: 133 us -> none  [one_axis_at_a_time(): return functools.reduce(lax.psum, axes, value)]
    pallas_call x0 -> x1, Pallas kernels: none -> 113 us  [call(): pl.pallas_call(functools.partial(kernel, ng, nz, count), out_shape=(jax.S...]
    all_gather x4 -> x0, waiting for transfers between devices: 112 us -> none  [all_blocks(): tiles = lax.all_gather(tiles, axes[k])]
    reduce_scatter x1 -> x0, waiting for transfers between devices: 55 us -> none  [body(): lax.psum_scatter(jnp.einsum('it,th->ih', spins, weighted, precision=lax.P...]
    all_to_all x3 -> x0, blocking collectives: 39.2 us -> none  [sent_to_all(): lax.all_to_all(jnp.broadcast_to(value[None], (size, *value.shape)), axis,...]
    dot_general x5 -> x0, matrix products: 37.8 us -> none  [the longest x2 16.2 us: body(): jnp.einsum('it,ih->th', spins, gather_axes(direction_w, SMP, (0, 1, 2), 0...]
    all_gather x2 -> x0, blocking collectives: 15.5 us -> none  [all_blocks(): tiles = lax.all_gather(tiles, axes[k])]
    all_to_all x2 -> x0, starting transfers between devices: 15.3 us -> none  [sent_to_all(): lax.all_to_all(jnp.broadcast_to(value[None], (size, *value.shape)), axis,...]
  transfers between devices with their start and end apart: 7 -> 0, of which waited for: 6 -> 0; matrix products, arithmetic and copies ran while one was open for 4% -> 0% of each run, Pallas kernels for 0% -> 0%
where the time goes in v1:
time: 116 us
  Pallas kernels  113 us (97%)
  local copies, waits for them, and re-layouts  2.85 us (2%)
    pallas_call x1, Pallas kernels, call(): pl.pallas_call(functools.partial(kernel, ng, nz, count), out_shape=(jax.S...  113 us
    unnamed x2, local copies, waits for them, and re-layouts  2.85 us

profile of v1, /device:TPU:1, one launch (start us, length us, event | category | flops | bytes accessed | tf_op | source)
XLA Modules:
  0.0 116.2 jit_solution(5966688873429203301)
XLA Ops:
  0.6 112.8 %step.1 = (f32[32,1024]{1,0:T(8,128)}, f32[8,128]{1,0:T(8,128)}) custom-call(s32[32,1024]{1,0:T(8,128)} %spk.1, bf16[1024,1024]{1,0:T(8,128)(2,1)} %w_hbm.1, f32[8,128]{1,0:T(8,128)} %bitcast.3, f32[32,1024]{1,0:T(8,128)} %fw.1, f32[8,128]{1,0:T(8,128)} %bitcast.4), custom_call_target="tpu_custom_call" | custom-call | tf_op jit(solution)/shard_map/step/pallas_call | solution.py:395
  113.4 1.6 %copy.9 = f32[32,1024]{1,0:T(8,128)} copy(f32[32,1024]{1,0:T(8,128)} %get-tuple-element.8) | data formatting | bytes 262144
  115.0 1.3 %copy.10 = f32[1024]{0:T(1024)} copy(f32[1024]{0:T(1024)} %bitcast.5) | data formatting | bytes 8192

commit v2 on v1

v2 whole, which is shorter than its diff:
```python
import functools

import jax
import jax.numpy as jnp
from jax import lax
from jax.experimental import pallas as pl
from jax.experimental.pallas import tpu as pltpu
from jax.sharding import PartitionSpec as P

MESH = pl.DeviceIdType.MESH
LAMBDA = 0.01
F32 = jnp.float32
BF16 = jnp.bfloat16
LANES = 128


def split(x):
    hi = x.astype(BF16)
    return hi, (x - hi.astype(F32)).astype(BF16)


def folded(x):
    rows, cols = x.shape
    tiles = [x[r : r + 8, k : k + LANES] for r in range(0, rows, 8) for k in range(0, cols, LANES)]
    return functools.reduce(lambda a, b: a + b, tiles)


def total(x):
    return jnp.sum(jnp.sum(x, axis=0, keepdims=True), axis=1, keepdims=True)


def row_of(x):
    return jnp.sum(x, axis=0, keepdims=True)


def added(parts):
    return functools.reduce(lambda a, b: a + b, parts)


def kernel(ng, nz, count, spk_h, w_h, hb_h, fw_h, fb_h, out_w_h, out_b_h,
           spk, fw, hb, fb, out_w, out_b, pk, wv, wt, fc, ft, sgn, hid, ch,
           vbuf, v1, v2, v3, v2s, v3s, w1, w2, w2s,
           p1s, p1, p2s, p2, p3s, p3, n1s, n1, n2s, n2, b1s, b1, b2s, b2, m1s, m1, x2s, x2, x3s, x3, w3s, w3,
           gb, gi, rs_s, rs_r, gall, gown, cols,
           local_sem, send, recv, near_sem, out_sem, on_sem, fx_sem, rs_sem, ag_sem):
    ns = 4 * nz
    tok = spk.shape[1]
    tiles = tok // LANES
    height = 32 * nz
    s = lax.axis_index("smp")
    g = lax.axis_index("grp")
    xh = s // (2 * nz)
    z = (s // 2) % nz
    c = s % 2
    q_me = 2 * xh + c
    q_core = 2 * xh + 1 - c
    q_x = 2 * (1 - xh) + c
    q_far = 2 * (1 - xh) + 1 - c
    core = s + 1 - 2 * c
    across = s + (2 * nz) * (1 - 2 * xh)

    def z_index(k):
        return 2 * nz * xh + 2 * k + c

    def remote(src, dst, ssem, rsem, dev):
        return pltpu.make_async_remote_copy(src_ref=src, dst_ref=dst, send_sem=ssem, recv_sem=rsem,
                                            device_id=dev, device_id_type=MESH)

    def peers(n, me, act, low=1, high=None):
        def step(j, carry):
            act(lax.rem(me + j, n))
            return carry
        lax.fori_loop(low, n if high is None else high, step, 0)

    def all_of(region, number, sent):
        move = remote(region, region, send.at[number], recv.at[number], {"smp": core})
        move.wait_send() if sent else move.wait_recv()

    class Exchange:
        def __init__(self, n, me, dev, src, dst, number, region):
            self.n, self.me, self.dev, self.src, self.dst = n, me, dev, src, dst
            self.number, self.region = number, region

        def start(self):
            peers(self.n, self.me, lambda p: remote(self.src(p), self.dst(self.me), send.at[self.number],
                                                    recv.at[self.number], self.dev(p)).start())

        def wait(self):
            all_of(self.region, self.number, False)

        def drain(self):
            all_of(self.region, self.number, True)

    def rows_of(buf, n, dst):
        return buf.at[pl.ds(0, n - 1)] if dst is None else dst

    def over_z(src, buf, number, dst=None, region=None):
        return Exchange(nz, z, lambda p: {"smp": z_index(p)}, src, dst or (lambda k: buf.at[k]), number,
                        rows_of(buf, nz, region))

    def over_grp(src, buf, number):
        return Exchange(ng, g, lambda p: {"grp": p}, src, lambda k: buf.at[k], number, rows_of(buf, ng, None))

    def quad_index(q):
        return 2 * nz * (q // 2) + 2 * z + q % 2

    def over_quad(src, buf, number):
        return Exchange(4, q_me, lambda p: {"smp": quad_index(p)}, src, lambda k: buf.at[k], number,
                        rows_of(buf, 4, None))

    plane = 4 * g + q_me
    quads = [quad_index(lax.rem(q_me + d, 4)) for d in range(4)]

    def over_all(do):
        for index in quads[1:]:
            do({"grp": g, "smp": index})

        def step(j, carry):
            h = lax.rem(g + j, ng)
            for index in quads:
                do({"grp": h, "smp": index})
            return carry
        lax.fori_loop(1, ng, step, 0)

    class Plane:
        def __init__(self, src, buf, number):
            self.src, self.buf, self.number = src, buf, number
            self.region = buf.at[pl.ds(0, 4 * ng - 1)]

        def start(self):
            over_all(lambda dev: remote(self.src, self.buf.at[plane], send.at[self.number], recv.at[self.number],
                                        dev).start())

        def wait(self):
            all_of(self.region, self.number, False)

        def drain(self):
            all_of(self.region, self.number, True)

    def lane(k, width=LANES):
        return pl.ds(pl.multiple_of(k * width, width), width)

    def block(k, size=32):
        return pl.ds(pl.multiple_of(k * size, size), size)

    loads = [pltpu.make_async_copy(a, b, local_sem.at[i]) for i, (a, b) in enumerate(
        ((spk_h, spk), (w_h.at[:, lane(z)], wv), (hb_h, hb), (fb_h, fb), (fw_h, fw)))]
    for load in loads:
        load.start()
    barrier = pltpu.get_barrier_semaphore()
    peers(nz, z, lambda p: pl.semaphore_signal(barrier, inc=1, device_id={"smp": z_index(p)}, device_id_type=MESH))
    over_all(lambda dev: pl.semaphore_signal(barrier, inc=1, device_id=dev, device_id_type=MESH))

    ex_fa = over_z(lambda p: fw.at[:, lane(p)], fc, 0, lambda k: fc.at[q_me, block(k)],
                   fc.at[q_me, pl.ds(0, 32 * (nz - 1))])
    ex_v1 = over_grp(lambda p: vbuf.at[p], v1, 1)
    ex_v2 = over_z(lambda p: v2s, v2, 2)
    ex_v3 = over_grp(lambda p: v3s, v3, 3)
    ex_w1 = over_grp(lambda p: vbuf.at[nz + p], w1, 4)
    ex_w2 = over_z(lambda p: w2s, w2, 5)
    ex_w3 = Plane(w3s, w3, 6)
    ex_p1 = over_grp(lambda p: p1s, p1, 7)
    ex_p2 = over_z(lambda p: p2s, p2, 8)
    ex_p3 = over_quad(lambda p: p3s, p3, 9)
    ex_n1 = Plane(n1s, n1, 10)
    ex_n2 = over_z(lambda p: n2s, n2, 11)
    ex_b1 = over_quad(lambda p: b1s, b1, 12)
    ex_b2 = over_z(lambda p: b2s, b2, 13)
    ex_m1 = Plane(m1s, m1, 29)
    ex_x2 = Plane(x2s, x2, 14)
    ex_x3 = over_z(lambda p: x3s, x3, 30)
    ex_gz = over_z(lambda p: gall.at[q_me, block(p)], gown, 15, lambda k: gown.at[:, lane(k)],
                   gown.at[:, pl.ds(0, LANES * (nz - 1))])

    def gather(buf, first, sems):
        to_core = remote(buf.at[q_me], buf.at[q_me], send.at[first], sems.at[0], {"smp": core})
        to_x = remote(buf.at[q_me], buf.at[q_me], send.at[first + 1], sems.at[1], {"smp": across})
        on = remote(buf.at[q_x], buf.at[q_x], send.at[first + 2], sems.at[2], {"smp": core})
        from_core = remote(buf.at[q_core], buf.at[q_core], send.at[first], sems.at[0], {"smp": core})
        from_x = remote(buf.at[q_x], buf.at[q_x], send.at[first + 1], sems.at[1], {"smp": across})
        from_on = remote(buf.at[q_far], buf.at[q_far], send.at[first + 2], sems.at[2], {"smp": core})
        return to_core, to_x, on, from_core, from_x, from_on

    fx = gather(fc, 16, fx_sem)
    ag = gather(gall, 19, ag_sem)

    piece = tok // ng
    up, down = lax.rem(z + 1, nz), lax.rem(z + nz - 1, nz)
    near = [remote(spk, pk.at[z], send.at[22 + i], near_sem.at[i], {"smp": z_index(k)})
            for i, k in enumerate((up, down))]
    from_near = [remote(spk, pk.at[k], send.at[22 + i], near_sem.at[i], {"smp": z_index(up)})
                 for i, k in enumerate((down, up))]

    def far_out(k):
        return remote(spk.at[:, lane(g, piece)], pk.at[z, :, lane(g, piece)], send.at[24], out_sem.at[z],
                      {"smp": z_index(k)})

    def far_first(k):
        part = pk.at[k, :, lane(g, piece)]
        return remote(part, part, send.at[24], out_sem.at[k], {"smp": z_index(k)})

    def far_on(k, h):
        part = pk.at[k, :, lane(g, piece)]
        return remote(part, part, send.at[25], on_sem.at[k], {"grp": h})

    def far_rest(k):
        part = pk.at[k, :, pl.ds(0, piece * (ng - 1))]
        return remote(part, part, send.at[25], on_sem.at[k], {"smp": core})

    bit = jnp.left_shift(jnp.int32(1), lax.broadcasted_iota(jnp.int32, (16, tok), 0)).astype(jnp.int16)

    def unpack(words, j):
        for xq in range(2):
            for cq in range(2):
                for k in range(nz):
                    row = words[pl.ds(2 * nz * xq + 2 * k + cq, 1), :]
                    at = ((2 * xq + cq) * nz + k) * 32
                    for half in range(2):
                        word = jnp.right_shift(row, 16 * half) if half else row
                        word = jnp.broadcast_to(word, (16, tok)).astype(jnp.int16)
                        sgn[pl.ds(at + 16 * half, 16), lane(j, tok)] = jnp.where(
                            jnp.bitwise_and(word, bit) != 0, BF16(1), BF16(-1))

    def hidden(j):
        pre = jnp.dot(wt[...], sgn[:, lane(j, tok)], preferred_element_type=F32)
        for r in range(tiles):
            part = pre[:, r * LANES : (r + 1) * LANES] + cols[0]
            hid[:, lane(j * tiles + r)] = jnp.tanh(part)

    loads[0].wait()
    unpack(spk, 0)
    loads[1].wait()
    loads[2].wait()
    loads[3].wait()
    cols[0] = jnp.broadcast_to(hb[pl.ds(z, 1), :], (LANES, LANES)).T
    cols[1] = jnp.broadcast_to(fb[pl.ds(z, 1), :], (LANES, LANES)).T
    for q in range(4):
        parts = [wv[pl.ds(32 * (2 * nz * (q // 2) + 2 * k + q % 2), 32), :] for k in range(nz)]
        wt[:, q * height : (q + 1) * height] = jnp.concatenate(parts, axis=0).astype(F32).T.astype(BF16)
    loads[4].wait()
    n1s[...] = row_of(folded(fw[...] * fw[...]) + folded(fb[...] * fb[...]) * F32(1.0 / ns))

    pl.semaphore_wait(barrier, nz - 1 + 4 * ng - 1)
    ex_fa.start()
    peers(nz, z, lambda k: far_out(k).start(), 2, nz - 1)
    for move in near:
        move.start()
    fc[q_me, block(z), :] = fw[:, lane(z)]
    hidden(0)
    ex_n1.start()
    n1[plane] = n1s[...]
    ex_fa.wait()
    fx[0].start()
    fx[1].start()

    def pass_on(k):
        far_first(k).wait_recv()
        peers(ng, g, lambda h: far_on(k, h).start())

    peers(nz, z, pass_on, 2, nz - 1)

    def shard(j):
        d = (j + 1) // 2
        return lax.rem(z + (2 * (j % 2) - 1) * d + nz, nz)

    def transposed(buf, q):
        hi, lo = split(buf[q].T)
        ft[:LANES, lane(q, height)] = hi
        ft[LANES:, lane(q, height)] = lo

    def values(j, base, col, first, width, more=False):
        k = shard(j)
        span = pl.ds(pl.multiple_of(first, 2 * height), width)
        res = jnp.dot(ft[:, span], sgn[span, lane(j, tok)], preferred_element_type=F32)
        for r in range(tiles):
            both = res[:LANES, r * LANES : (r + 1) * LANES] + res[LANES:, r * LANES : (r + 1) * LANES]
            if col is not None:
                both = both + cols[col]
            got = row_of(both * hid[:, lane(j * tiles + r)])
            at = (base + k, pl.ds(r, 1), slice(None))
            vbuf[at] = vbuf[at] + got if more else got

    def each(low, high, act):
        def step(j, carry):
            act(j)
            return carry
        lax.fori_loop(low, high, step, 0)

    for i in (1, 0):
        from_near[i].wait_recv()
        unpack(pk.at[(down, up)[i]], 2 - i)
        hidden(2 - i)
    fx[4].wait_recv()
    fx[2].start()
    fx[3].wait_recv()
    transposed(fc, q_me)
    transposed(fc, q_core)
    transposed(fc, q_x)
    fx[5].wait_recv()
    transposed(fc, q_far)
    each(0, 3, lambda j: values(j, 0, 1, 0, 4 * height))

    def arrive(j):
        k = shard(j)
        far_rest(k).wait_recv()
        unpack(pk.at[k], j)
        hidden(j)
        values(j, 0, 1, 0, 4 * height)

    each(3, nz, arrive)

    ex_v1.start()
    p1s[...] = row_of(added([vbuf[k] for k in range(nz)]))
    ex_p1.start()
    v1[g] = vbuf[g]
    p1[g] = p1s[...]
    ex_n1.wait()
    n2s[...] = added([n1[k] for k in range(4 * ng)])
    ex_n2.start()
    n2[z] = n2s[...]
    ex_v1.wait()
    v2s[...] = added([v1[k] for k in range(ng)])
    ex_v2.start()
    ex_p1.wait()
    p2s[...] = added([p1[k] for k in range(ng)])
    ex_p2.start()
    v2[z] = v2s[...]
    p2[z] = p2s[...]
    ex_fa.drain()
    ex_v1.drain()
    ex_p1.drain()
    ex_n1.drain()
    for move in near:
        move.wait_send()
    peers(nz, z, lambda k: far_out(k).wait_send(), 2, nz - 1)
    ex_v2.wait()
    v3s[...] = added([v2[k] for k in range(nz)])
    ex_v3.start()
    ex_p2.wait()
    p3s[...] = added([p2[k] for k in range(nz)])
    ex_p3.start()
    v3[g] = v3s[...]
    p3[q_me] = p3s[...]
    ex_v2.drain()
    ex_p2.drain()
    peers(nz, z, lambda k: far_rest(k).wait_send(), 2, nz - 1)
    ex_v3.wait()
    ex_p3.wait()
    inv = F32(1.0 / count)
    mean = total(added([p3[k] for k in range(4)])) * inv
    gb[...] = jnp.zeros((LANES, LANES), F32)

    def weigh(j):
        own = v3[shard(j)] - mean
        bias = gb[...]
        for r in range(tiles):
            prod = hid[:, lane(j * tiles + r)] * own[r : r + 1, :]
            hi, lo = split(prod)
            ch[:LANES, lane(j * tiles + r)] = hi
            ch[LANES:, lane(j * tiles + r)] = lo
            bias = bias + prod
        gb[...] = bias

    each(0, nz, weigh)

    once = (s + ns) // ns

    def image(q, slot):
        def run(_):
            res = lax.dot_general(sgn[block(q, height), :], ch[...], (((1,), (1,)), ((), ())),
                                  preferred_element_type=F32)
            gi[slot] = res[:, :LANES] + res[:, LANES:]
        each(0, once, run)

    hop0 = remote(gi.at[0], rs_r.at[0], send.at[26], rs_sem.at[0], {"smp": core})
    hop1 = remote(rs_s, rs_r.at[1], send.at[27], rs_sem.at[1], {"smp": across})
    hop2 = remote(gi.at[1], rs_r.at[2], send.at[28], rs_sem.at[2], {"smp": core})
    image(q_far, 0)
    hop0.start()
    image(q_x, 2)
    b1s[...] = row_of(gb[...].T)
    off = v3s[...] - mean
    m1s[...] = row_of(off * off)
    ex_b1.start()
    b1[q_me] = b1s[...]
    hop0.wait_recv()
    rs_s[...] = gi[2] + rs_r[0]
    hop1.start()
    image(q_core, 1)
    hop2.start()
    ex_m1.start()
    m1[plane] = m1s[...]
    image(q_me, 3)
    ex_b1.wait()
    b2s[...] = added([b1[k] for k in range(4)])
    ex_b2.start()
    b2[z] = b2s[...]
    cols[2] = jnp.broadcast_to(b2s[...], (LANES, LANES)).T
    ex_v3.drain()
    ex_p3.drain()
    ex_b1.drain()
    ex_n2.wait()
    ex_n2.drain()
    norm0 = total(added([n2[k] for k in range(nz)]))
    hop2.wait_recv()
    gi[3] = gi[3] + rs_r[2]
    hop1.wait_recv()
    gall[q_me] = gi[3] + rs_r[1]
    ag[1].start()
    ag[0].start()
    ex_gz.start()
    gown[:, lane(z)] = gall[q_me, block(z), :]
    transposed(gall, q_me)
    ag[3].wait_recv()
    transposed(gall, q_core)
    each(0, nz, lambda j: values(j, nz, 2, xh * 2 * height, 2 * height))

    ex_b2.wait()
    ex_m1.wait()
    for k in range(nz):
        gb[pl.ds(k, 1), :] = b2[k]
    if nz < 8:
        gb[nz:8, :] = jnp.zeros((8 - nz, LANES), F32)
    image_b = gb[:8, :]
    curvature = total(added([m1[k] for k in range(4 * ng)])) * inv + F32(LAMBDA) * norm0
    alpha0 = norm0 / curvature
    res_b = fb[...] - alpha0 * (image_b * inv + F32(LAMBDA) * fb[...])
    own_f = fc[q_me]
    res_w = own_f - alpha0 * (gall[q_me] * inv + F32(LAMBDA) * own_f)
    x2s[0:1] = row_of(folded(res_w * res_w) + res_b * res_b * F32(1.0 / ns))
    x2s[1:2] = row_of(folded(res_w * own_f) + res_b * fb[...] * F32(1.0 / ns))
    ex_x2.start()
    x2[plane] = x2s[...]
    ag[4].wait_recv()
    ag[2].start()
    transposed(gall, q_x)
    ag[5].wait_recv()
    transposed(gall, q_far)
    each(0, nz, lambda j: values(j, nz, None, (1 - xh) * 2 * height, 2 * height, True))

    ex_w1.start()
    w1[g] = vbuf[nz + g]
    ex_x2.wait()
    x3s[...] = added([x2[k] for k in range(4 * ng)])
    ex_x3.start()
    x3[z] = x3s[...]
    for move in (*fx[:3], *ag[:3], hop0, hop1, hop2):
        move.wait_send()
    for ex in (ex_m1, ex_b2, ex_gz):
        ex.drain()
    ex_gz.wait()
    ex_w1.wait()
    w2s[...] = added([w1[k] for k in range(ng)])
    ex_w2.start()
    w2[z] = w2s[...]
    ex_w1.drain()
    ex_x2.drain()
    ex_x3.wait()
    ex_x3.drain()
    sums = added([x3[k] for k in range(nz)])
    norm1 = total(sums[0:1])
    cross = total(sums[1:2])
    beta = norm1 / norm0
    scale_f = F32(1.0) - alpha0 * F32(LAMBDA) + beta
    norm_d = norm1 + F32(2.0) * beta * cross + beta * beta * norm0
    ex_w2.wait()
    mixed = scale_f * off - (alpha0 * inv) * added([w2[k] for k in range(nz)])
    here = total(mixed)
    spread = mixed - here * F32(1.0 / tok)
    w3s[0:1] = jnp.broadcast_to(here, (1, LANES))
    w3s[1:2] = row_of(spread * spread)
    ex_w3.start()
    w3[plane] = w3s[...]
    ex_w2.drain()
    ex_w3.wait()
    shards = [w3[k, 0:1, :] for k in range(4 * ng)]
    mean1 = added(shards) * inv
    between = row_of(jnp.zeros((1, LANES), F32))
    for one in shards:
        gap = one * F32(1.0 / tok) - mean1
        between += gap * gap
    within = total(added([w3[k, 1:2, :] for k in range(4 * ng)]))
    square = within + between[:, 0:1] * F32(tok)
    curvature = square * inv + F32(LAMBDA) * norm_d
    alpha1 = norm1 / curvature
    factor_f = alpha0 + alpha1 * scale_f
    factor_g = alpha1 * alpha0 * inv
    out_w[...] = factor_f * fw[...] - factor_g * gown[...]
    out_b[...] = factor_f * fb[...] - factor_g * image_b
    stores = [pltpu.make_async_copy(a, b, local_sem.at[5 + i]) for i, (a, b) in enumerate(
        ((out_w, out_w_h), (out_b, out_b_h)))]
    for store in stores:
        store.start()
    ex_w3.drain()
    for store in stores:
        store.wait()


def call(ng, nz, count, spk, w, hb, fw, fb):
    ns = 4 * nz
    tok = spk.shape[1]
    words, height = spk.shape[0], 32 * nz
    nv = 32 * words
    tile = (8, LANES)
    dma = pltpu.SemaphoreType.DMA
    anywhere = pl.BlockSpec(memory_space=pl.ANY)

    def f32(*shape):
        return pltpu.VMEM(shape, F32)

    scratch = [
        pltpu.VMEM((words, tok), jnp.int32), f32(*fw.shape), f32(*tile), f32(*tile), f32(*fw.shape), f32(*tile),
        pltpu.VMEM((nz, words, tok), jnp.int32),
        pltpu.VMEM((nv, LANES), BF16),
        pltpu.VMEM((LANES, nv), BF16),
        f32(4, height, LANES),
        pltpu.VMEM((2 * LANES, nv), BF16),
        pltpu.VMEM((nv, nz * tok), BF16),
        f32(LANES, nz * tok),
        pltpu.VMEM((2 * LANES, nz * tok), BF16),
        f32(2 * nz, *tile), f32(ng, *tile), f32(nz, *tile), f32(ng, *tile), f32(*tile), f32(*tile),
        f32(ng, *tile), f32(nz, *tile), f32(*tile),
        f32(1, LANES), f32(ng, 1, LANES), f32(1, LANES), f32(nz, 1, LANES), f32(1, LANES), f32(4, 1, LANES),
        f32(1, LANES), f32(4 * ng, 1, LANES), f32(1, LANES), f32(nz, 1, LANES),
        f32(1, LANES), f32(4, 1, LANES), f32(1, LANES), f32(nz, 1, LANES), f32(1, LANES), f32(4 * ng, 1, LANES),
        f32(2, LANES), f32(4 * ng, 2, LANES), f32(2, LANES), f32(nz, 2, LANES), f32(2, LANES), f32(4 * ng, 2, LANES),
        f32(LANES, LANES), f32(4, height, LANES), f32(height, LANES), f32(3, height, LANES), f32(4, height, LANES),
        f32(32, nz * LANES), f32(3, LANES, LANES),
        dma((7,)), dma((31,)), dma((31,)), dma((2,)), dma((nz,)), dma((nz,)), dma((3,)), dma((3,)), dma((3,)),
    ]
    return pl.pallas_call(
        functools.partial(kernel, ng, nz, count),
        out_shape=(jax.ShapeDtypeStruct(fw.shape, F32), jax.ShapeDtypeStruct(tile, F32)),
        in_specs=[anywhere] * 5,
        out_specs=(anywhere, anywhere),
        scratch_shapes=scratch,
        compiler_params=pltpu.CompilerParams(collective_id=0, has_side_effects=True,
                                             vmem_limit_bytes=60 * 1024 * 1024),
        name="step",
    )(spk, w, hb, fw, fb)


def solution(mesh):
    ng, ns = mesh.shape["grp"], mesh.shape["smp"]
    nz = ns // 4

    def body(spk, w, hb, fw, fb):
        count = spk.shape[1] * ns
        tile = (8, LANES)
        pad = 8 * LANES - hb.shape[0]
        hb, fb = (jnp.pad(v, (0, pad)).reshape(tile) for v in (hb, fb))
        out_w, out_b = call(ng, nz, count, spk, w, hb, fw, fb)
        return out_w, out_b.reshape(-1)[: nz * LANES]

    return jax.shard_map(body, mesh=mesh,
                         in_specs=(P(None, "smp"), P(None, "grp"), P("grp"), P("smp", "grp"), P("grp")),
                         out_specs=(P("smp", "grp"), P("grp")), check_vma=False)
```

time: 116 us -> 87.3 us (0.75)
  Pallas kernels: 113 us -> 83.6 us
    pallas_call x1, Pallas kernels: 113 us -> 83.6 us  [call(): pl.pallas_call(functools.partial(kernel, ng, nz, count), out_shape=(jax.S...]
where the time goes in v2:
time: 87.3 us; the launch traced here: 87.1 us
  Pallas kernels  83.6 us (96%)
  local copies, waits for them, and re-layouts  2.85 us (3%)
    pallas_call x1, Pallas kernels, call(): pl.pallas_call(functools.partial(kernel, ng, nz, count), out_shape=(jax.S...  83.6 us
    unnamed x2, local copies, waits for them, and re-layouts  2.85 us

profile of v2, /device:TPU:1, one launch (start us, length us, event | category | flops | bytes accessed | tf_op | source)
XLA Modules:
  0.0 87.1 jit_solution(12003753222903370124)
XLA Ops:
  0.6 83.6 %step.1 = (f32[32,1024]{1,0:T(8,128)}, f32[8,128]{1,0:T(8,128)}) custom-call(s32[32,1024]{1,0:T(8,128)} %spk_h.1, bf16[1024,1024]{1,0:T(8,128)(2,1)} %w_h.1, f32[8,128]{1,0:T(8,128)} %bitcast.3, f32[32,1024]{1,0:T(8,128)} %fw_h.1, f32[8,128]{1,0:T(8,128)} %bitcast.4), custom_call_target="tpu_custom_call" | custom-call | tf_op jit(solution)/shard_map/step/pallas_call | solution.py:531
  84.3 1.6 %copy.9 = f32[32,1024]{1,0:T(8,128)} copy(f32[32,1024]{1,0:T(8,128)} %get-tuple-element.8) | data formatting | bytes 262144
  85.9 1.3 %copy.10 = f32[1024]{0:T(1024)} copy(f32[1024]{0:T(1024)} %bitcast.5) | data formatting | bytes 8192

commit v3 on v2

--- a/solution.py
+++ b/solution.py
@@ -42,7 +42,7 @@
            vbuf, v1, v2, v3, v2s, v3s, w1, w2, w2s,
            p1s, p1, p2s, p2, p3s, p3, n1s, n1, n2s, n2, b1s, b1, b2s, b2, m1s, m1, x2s, x2, x3s, x3, w3s, w3,
            gb, gi, rs_s, rs_r, gall, gown, cols,
-           local_sem, send, recv, near_sem, out_sem, on_sem, fx_sem, rs_sem, ag_sem):
+           local_sem, send, recv, near_sem, fa_sem, out_sem, on_sem, fx_sem, rs_sem, ag_sem):
     ns = 4 * nz
     tok = spk.shape[1]
     tiles = tok // LANES
@@ -151,8 +151,6 @@
     peers(nz, z, lambda p: pl.semaphore_signal(barrier, inc=1, device_id={"smp": z_index(p)}, device_id_type=MESH))
     over_all(lambda dev: pl.semaphore_signal(barrier, inc=1, device_id=dev, device_id_type=MESH))
 
-    ex_fa = over_z(lambda p: fw.at[:, lane(p)], fc, 0, lambda k: fc.at[q_me, block(k)],
-                   fc.at[q_me, pl.ds(0, 32 * (nz - 1))])
     ex_v1 = over_grp(lambda p: vbuf.at[p], v1, 1)
     ex_v2 = over_z(lambda p: v2s, v2, 2)
     ex_v3 = over_grp(lambda p: v3s, v3, 3)
@@ -182,7 +180,6 @@
         return to_core, to_x, on, from_core, from_x, from_on
 
     fx = gather(fc, 16, fx_sem)
-    ag = gather(gall, 19, ag_sem)
 
     piece = tok // ng
     up, down = lax.rem(z + 1, nz), lax.rem(z + nz - 1, nz)
@@ -190,6 +187,18 @@
             for i, k in enumerate((up, down))]
     from_near = [remote(spk, pk.at[k], send.at[22 + i], near_sem.at[i], {"smp": z_index(up)})
                  for i, k in enumerate((down, up))]
+
+    def force_out(k):
+        return remote(fw.at[:, lane(k)], fc.at[q_me, block(z)], send.at[0], fa_sem.at[z], {"smp": z_index(k)})
+
+    def force_in(k):
+        part = fc.at[q_me, block(k)]
+        return remote(part, part, send.at[0], fa_sem.at[k], {"smp": z_index(k)})
+
+    def force_on(k):
+        part = fc.at[q_me, block(k)]
+        remote(part, part, send.at[17], fx_sem.at[1], {"smp": across}).start()
+        remote(part, part, send.at[16], fx_sem.at[0], {"smp": core}).start()
 
     def far_out(k):
         return remote(spk.at[:, lane(g, piece)], pk.at[z, :, lane(g, piece)], send.at[24], out_sem.at[z],
@@ -241,7 +250,7 @@
     n1s[...] = row_of(folded(fw[...] * fw[...]) + folded(fb[...] * fb[...]) * F32(1.0 / ns))
 
     pl.semaphore_wait(barrier, nz - 1 + 4 * ng - 1)
-    ex_fa.start()
+    peers(nz, z, lambda k: force_out(k).start())
     peers(nz, z, lambda k: far_out(k).start(), 2, nz - 1)
     for move in near:
         move.start()
@@ -249,36 +258,9 @@
     hidden(0)
     ex_n1.start()
     n1[plane] = n1s[...]
-    ex_fa.wait()
-    fx[0].start()
-    fx[1].start()
-
-    def pass_on(k):
-        far_first(k).wait_recv()
-        peers(ng, g, lambda h: far_on(k, h).start())
-
-    peers(nz, z, pass_on, 2, nz - 1)
-
     def shard(j):
         d = (j + 1) // 2
         return lax.rem(z + (2 * (j % 2) - 1) * d + nz, nz)
-
-    def transposed(buf, q):
-        hi, lo = split(buf[q].T)
-        ft[:LANES, lane(q, height)] = hi
-        ft[LANES:, lane(q, height)] = lo
-
-    def values(j, base, col, first, width, more=False):
-        k = shard(j)
-        span = pl.ds(pl.multiple_of(first, 2 * height), width)
-        res = jnp.dot(ft[:, span], sgn[span, lane(j, tok)], preferred_element_type=F32)
-        for r in range(tiles):
-            both = res[:LANES, r * LANES : (r + 1) * LANES] + res[LANES:, r * LANES : (r + 1) * LANES]
-            if col is not None:
-                both = both + cols[col]
-            got = row_of(both * hid[:, lane(j * tiles + r)])
-            at = (base + k, pl.ds(r, 1), slice(None))
-            vbuf[at] = vbuf[at] + got if more else got
 
     def each(low, high, act):
         def step(j, carry):
@@ -286,28 +268,64 @@
             return carry
         lax.fori_loop(low, high, step, 0)
 
+    force_on(z)
+
+    def force_pass(j):
+        force_in(shard(j)).wait_recv()
+        force_on(shard(j))
+
+    each(1, nz, force_pass)
+
+    def pass_on(j):
+        k = shard(j)
+        far_first(k).wait_recv()
+        peers(ng, g, lambda h: far_on(k, h).start())
+
+    each(3, nz, pass_on)
+
+    def transposed(buf, q):
+        hi, lo = split(buf[q].T)
+        ft[:LANES, lane(q, height)] = hi
+        ft[LANES:, lane(q, height)] = lo
+
+    def values(wide, i, base, col, rows, more=False):
+        res = jnp.dot(ft[:, rows], sgn[rows, lane(i, wide * tok)], preferred_element_type=F32)
+        for n in range(wide):
+            k = shard(i * wide + n)
+            for r in range(tiles):
+                at = (n * tiles + r) * LANES
+                both = res[:LANES, at : at + LANES] + res[LANES:, at : at + LANES]
+                if col is not None:
+                    both = both + cols[col]
+                got = row_of(both * hid[:, lane((i * wide + n) * tiles + r)])
+                to = (base + k, pl.ds(r, 1), slice(None))
+                vbuf[to] = vbuf[to] + got if more else got
+
     for i in (1, 0):
         from_near[i].wait_recv()
         unpack(pk.at[(down, up)[i]], 2 - i)
         hidden(2 - i)
+    def arrive(j):
+        k = shard(j)
+        far_rest(k).wait_recv()
+        unpack(pk.at[k], j)
+        hidden(j)
+
     fx[4].wait_recv()
     fx[2].start()
     fx[3].wait_recv()
     transposed(fc, q_me)
     transposed(fc, q_core)
     transposed(fc, q_x)
+    early = min(nz, 5)
+    each(3, early, arrive)
     fx[5].wait_recv()
     transposed(fc, q_far)
-    each(0, 3, lambda j: values(j, 0, 1, 0, 4 * height))
-
-    def arrive(j):
-        k = shard(j)
-        far_rest(k).wait_recv()
-        unpack(pk.at[k], j)
-        hidden(j)
-        values(j, 0, 1, 0, 4 * height)
-
-    each(3, nz, arrive)
+    every = pl.ds(0, 4 * height)
+    wide = nz // 2
+    values(wide, 0, 0, 1, every)
+    each(early, nz, arrive)
+    values(wide, 1, 0, 1, every)
 
     ex_v1.start()
     p1s[...] = row_of(added([vbuf[k] for k in range(nz)]))
@@ -326,7 +344,7 @@
     ex_p2.start()
     v2[z] = v2s[...]
     p2[z] = p2s[...]
-    ex_fa.drain()
+    peers(nz, z, lambda k: force_out(k).wait_send())
     ex_v1.drain()
     ex_p1.drain()
     ex_n1.drain()
@@ -348,72 +366,90 @@
     ex_p3.wait()
     inv = F32(1.0 / count)
     mean = total(added([p3[k] for k in range(4)])) * inv
-    gb[...] = jnp.zeros((LANES, LANES), F32)
-
-    def weigh(j):
-        own = v3[shard(j)] - mean
-        bias = gb[...]
-        for r in range(tiles):
-            prod = hid[:, lane(j * tiles + r)] * own[r : r + 1, :]
-            hi, lo = split(prod)
-            ch[:LANES, lane(j * tiles + r)] = hi
-            ch[LANES:, lane(j * tiles + r)] = lo
-            bias = bias + prod
+    once = (s + ns) // ns
+
+    def first_rows(_):
+        bias = jnp.zeros((LANES, LANES), F32)
+        sums = [None, None]
+        for j in range(nz):
+            own = v3[shard(j)] - mean
+            for r in range(tiles):
+                at = (j * tiles + r) * LANES
+                prod = hid[:, at : at + LANES] * own[r : r + 1, :]
+                hi, lo = split(prod)
+                ch[:LANES, at : at + LANES] = hi
+                ch[LANES:, at : at + LANES] = lo
+                bias = bias + prod
+            span = slice(j * tok, (j + 1) * tok)
+            for h in range(2):
+                res = lax.dot_general(sgn[h * height : (h + 1) * height, span], ch[:, span],
+                                      (((1,), (1,)), ((), ())), preferred_element_type=F32)
+                sums[h] = res if sums[h] is None else sums[h] + res
+        for h in range(2):
+            gi[h] = sums[h][:, :LANES] + sums[h][:, LANES:]
         gb[...] = bias
 
-    each(0, nz, weigh)
-
-    once = (s + ns) // ns
-
-    def image(q, slot):
+    each(0, once, first_rows)
+
+    def image(q):
         def run(_):
             res = lax.dot_general(sgn[block(q, height), :], ch[...], (((1,), (1,)), ((), ())),
                                   preferred_element_type=F32)
-            gi[slot] = res[:, :LANES] + res[:, LANES:]
+            gi[q] = res[:, :LANES] + res[:, LANES:]
         each(0, once, run)
 
-    hop0 = remote(gi.at[0], rs_r.at[0], send.at[26], rs_sem.at[0], {"smp": core})
-    hop1 = remote(rs_s, rs_r.at[1], send.at[27], rs_sem.at[1], {"smp": across})
-    hop2 = remote(gi.at[1], rs_r.at[2], send.at[28], rs_sem.at[2], {"smp": core})
-    image(q_far, 0)
-    hop0.start()
-    image(q_x, 2)
+    mine = (c, 2 + c)
+    other = (1 - c, 3 - c)
+    to_core = [remote(gi.at[other[i]], rs_r.at[i], send.at[26 + i], rs_sem.at[i], {"smp": core}) for i in range(2)]
+    to_x = [remote(rs_s.at[i], rs_r.at[2 + i], send.at[19 + i], rs_sem.at[2 + i], {"smp": across}) for i in range(2)]
+    share = [remote(gall.at[mine[i]], gall.at[mine[i]], send.at[21 + 7 * i], ag_sem.at[i], {"smp": core})
+             for i in range(2)]
+    shared = [remote(gall.at[other[i]], gall.at[other[i]], send.at[21 + 7 * i], ag_sem.at[i], {"smp": core})
+              for i in range(2)]
+    to_core[0].start()
+    image(other[1])
+    to_core[1].start()
     b1s[...] = row_of(gb[...].T)
     off = v3s[...] - mean
     m1s[...] = row_of(off * off)
     ex_b1.start()
     b1[q_me] = b1s[...]
-    hop0.wait_recv()
-    rs_s[...] = gi[2] + rs_r[0]
-    hop1.start()
-    image(q_core, 1)
-    hop2.start()
+    to_core[0].wait_recv()
+    rs_s[0] = gi[mine[0]] + rs_r[0]
+    to_x[0].start()
+    image(mine[1])
+    to_core[1].wait_recv()
+    rs_s[1] = gi[mine[1]] + rs_r[1]
+    to_x[1].start()
     ex_m1.start()
     m1[plane] = m1s[...]
-    image(q_me, 3)
+    ex_v3.drain()
+    ex_p3.drain()
+    ex_n2.wait()
+    ex_n2.drain()
+    norm0 = total(added([n2[k] for k in range(nz)]))
     ex_b1.wait()
     b2s[...] = added([b1[k] for k in range(4)])
     ex_b2.start()
     b2[z] = b2s[...]
     cols[2] = jnp.broadcast_to(b2s[...], (LANES, LANES)).T
-    ex_v3.drain()
-    ex_p3.drain()
     ex_b1.drain()
-    ex_n2.wait()
-    ex_n2.drain()
-    norm0 = total(added([n2[k] for k in range(nz)]))
-    hop2.wait_recv()
-    gi[3] = gi[3] + rs_r[2]
-    hop1.wait_recv()
-    gall[q_me] = gi[3] + rs_r[1]
-    ag[1].start()
-    ag[0].start()
+
+    def quarter(q, first=False):
+        transposed(gall, q)
+        each(0, 2, lambda i: values(wide, i, nz, 2 if first else None, block(q, height), not first))
+
+    to_x[0].wait_recv()
+    gall[mine[0]] = rs_s[0] + rs_r[2]
+    share[0].start()
+    quarter(mine[0], True)
+    shared[0].wait_recv()
+    quarter(other[0])
+    to_x[1].wait_recv()
+    gall[mine[1]] = rs_s[1] + rs_r[3]
+    share[1].start()
     ex_gz.start()
     gown[:, lane(z)] = gall[q_me, block(z), :]
-    transposed(gall, q_me)
-    ag[3].wait_recv()
-    transposed(gall, q_core)
-    each(0, nz, lambda j: values(j, nz, 2, xh * 2 * height, 2 * height))
 
     ex_b2.wait()
     ex_m1.wait()
@@ -431,12 +467,9 @@
     x2s[1:2] = row_of(folded(res_w * own_f) + res_b * fb[...] * F32(1.0 / ns))
     ex_x2.start()
     x2[plane] = x2s[...]
-    ag[4].wait_recv()
-    ag[2].start()
-    transposed(gall, q_x)
-    ag[5].wait_recv()
-    transposed(gall, q_far)
-    each(0, nz, lambda j: values(j, nz, None, (1 - xh) * 2 * height, 2 * height, True))
+    quarter(mine[1])
+    shared[1].wait_recv()
+    quarter(other[1])
 
     ex_w1.start()
     w1[g] = vbuf[nz + g]
@@ -444,7 +477,7 @@
     x3s[...] = added([x2[k] for k in range(4 * ng)])
     ex_x3.start()
     x3[z] = x3s[...]
-    for move in (*fx[:3], *ag[:3], hop0, hop1, hop2):
+    for move in (*fx[:3], *to_core, *to_x, *share):
         move.wait_send()
     for ex in (ex_m1, ex_b2, ex_gz):
         ex.drain()
@@ -524,9 +557,9 @@
         f32(1, LANES), f32(4 * ng, 1, LANES), f32(1, LANES), f32(nz, 1, LANES),
         f32(1, LANES), f32(4, 1, LANES), f32(1, LANES), f32(nz, 1, LANES), f32(1, LANES), f32(4 * ng, 1, LANES),
         f32(2, LANES), f32(4 * ng, 2, LANES), f32(2, LANES), f32(nz, 2, LANES), f32(2, LANES), f32(4 * ng, 2, LANES),
-        f32(LANES, LANES), f32(4, height, LANES), f32(height, LANES), f32(3, height, LANES), f32(4, height, LANES),
+        f32(LANES, LANES), f32(4, height, LANES), f32(2, height, LANES), f32(4, height, LANES), f32(4, height, LANES),
         f32(32, nz * LANES), f32(3, LANES, LANES),
-        dma((7,)), dma((31,)), dma((31,)), dma((2,)), dma((nz,)), dma((nz,)), dma((3,)), dma((3,)), dma((3,)),
+        dma((7,)), dma((31,)), dma((31,)), dma((2,)), dma((nz,)), dma((nz,)), dma((nz,)), dma((3,)), dma((4,)), dma((2,)),
     ]
     return pl.pallas_call(
         functools.partial(kernel, ng, nz, count),

time: 87.3 us -> 82.9 us (0.950)
  Pallas kernels: 83.6 us -> 79.3 us
    pallas_call x1, Pallas kernels: 83.6 us -> 79.3 us  [call(): pl.pallas_call(functools.partial(kernel, ng, nz, count), out_shape=(jax.S...]
where the time goes in v3:
time: 82.9 us; the launch traced here: 82.8 us
  Pallas kernels  79.3 us (96%)
  local copies, waits for them, and re-layouts  2.85 us (3%)
    pallas_call x1, Pallas kernels, call(): pl.pallas_call(functools.partial(kernel, ng, nz, count), out_shape=(jax.S...  79.3 us
    unnamed x2, local copies, waits for them, and re-layouts  2.85 us

profile of v3, /device:TPU:1, one launch (start us, length us, event | category | flops | bytes accessed | tf_op | source)
XLA Modules:
  0.0 82.8 jit_solution(7965090578129928211)
XLA Ops:
  0.6 79.3 %step.1 = (f32[32,1024]{1,0:T(8,128)}, f32[8,128]{1,0:T(8,128)}) custom-call(s32[32,1024]{1,0:T(8,128)} %spk_h.1, bf16[1024,1024]{1,0:T(8,128)(2,1)} %w_h.1, f32[8,128]{1,0:T(8,128)} %bitcast.3, f32[32,1024]{1,0:T(8,128)} %fw_h.1, f32[8,128]{1,0:T(8,128)} %bitcast.4), custom_call_target="tpu_custom_call" | custom-call | tf_op jit(solution)/shard_map/step/pallas_call | solution.py:564
  79.9 1.6 %copy.9 = f32[32,1024]{1,0:T(8,128)} copy(f32[32,1024]{1,0:T(8,128)} %get-tuple-element.8) | data formatting | bytes 262144
  81.5 1.3 %copy.10 = f32[1024]{0:T(1024)} copy(f32[1024]{0:T(1024)} %bitcast.5) | data formatting | bytes 8192

commit v4 on v3

--- a/solution.py
+++ b/solution.py
@@ -138,7 +138,7 @@
             all_of(self.region, self.number, True)
 
     def lane(k, width=LANES):
-        return pl.ds(pl.multiple_of(k * width, width), width)
+        return pl.ds(k * width if isinstance(k, int) else pl.multiple_of(k * width, width), width)
 
     def block(k, size=32):
         return pl.ds(pl.multiple_of(k * size, size), size)
@@ -268,6 +268,8 @@
             return carry
         lax.fori_loop(low, high, step, 0)
 
+    once = (s + ns) // ns
+
     force_on(z)
 
     def force_pass(j):
@@ -288,16 +290,17 @@
         ft[:LANES, lane(q, height)] = hi
         ft[LANES:, lane(q, height)] = lo
 
-    def values(wide, i, base, col, rows, more=False):
-        res = jnp.dot(ft[:, rows], sgn[rows, lane(i, wide * tok)], preferred_element_type=F32)
+    def values(slot, wide, base, col, rows, more=False):
+        span = pl.ds(slot * tok, wide * tok)
+        res = jnp.dot(ft[:, rows], sgn[rows, span], preferred_element_type=F32)
         for n in range(wide):
-            k = shard(i * wide + n)
+            k = shard(slot + n)
             for r in range(tiles):
                 at = (n * tiles + r) * LANES
                 both = res[:LANES, at : at + LANES] + res[LANES:, at : at + LANES]
                 if col is not None:
                     both = both + cols[col]
-                got = row_of(both * hid[:, lane((i * wide + n) * tiles + r)])
+                got = row_of(both * hid[:, lane((slot + n) * tiles + r)])
                 to = (base + k, pl.ds(r, 1), slice(None))
                 vbuf[to] = vbuf[to] + got if more else got
 
@@ -317,15 +320,24 @@
     transposed(fc, q_me)
     transposed(fc, q_core)
     transposed(fc, q_x)
-    early = min(nz, 5)
+    early = 3 if nz == 4 else 5
     each(3, early, arrive)
     fx[5].wait_recv()
     transposed(fc, q_far)
     every = pl.ds(0, 4 * height)
-    wide = nz // 2
-    values(wide, 0, 0, 1, every)
-    each(early, nz, arrive)
-    values(wide, 1, 0, 1, every)
+    values(0, 3, 0, 1, every)
+    for j in range(early, nz):
+        far_rest(shard(j)).wait_recv()
+
+    def overlap(_):
+        for j in range(early, nz):
+            unpack(pk.at[shard(j)], j)
+            if j == early and early > 3:
+                values(3, early - 3, 0, 1, every)
+            hidden(j)
+
+    each(0, once, overlap)
+    values(early, nz - early, 0, 1, every)
 
     ex_v1.start()
     p1s[...] = row_of(added([vbuf[k] for k in range(nz)]))
@@ -366,7 +378,8 @@
     ex_p3.wait()
     inv = F32(1.0 / count)
     mean = total(added([p3[k] for k in range(4)])) * inv
-    once = (s + ns) // ns
+    mine = (c, 2 + c)
+    other = (1 - c, 3 - c)
 
     def first_rows(_):
         bias = jnp.zeros((LANES, LANES), F32)
@@ -381,12 +394,11 @@
                 ch[LANES:, at : at + LANES] = lo
                 bias = bias + prod
             span = slice(j * tok, (j + 1) * tok)
-            for h in range(2):
-                res = lax.dot_general(sgn[h * height : (h + 1) * height, span], ch[:, span],
-                                      (((1,), (1,)), ((), ())), preferred_element_type=F32)
-                sums[h] = res if sums[h] is None else sums[h] + res
-        for h in range(2):
-            gi[h] = sums[h][:, :LANES] + sums[h][:, LANES:]
+            res = lax.dot_general(sgn[block(other[0], height), span], ch[:, span],
+                                  (((1,), (1,)), ((), ())), preferred_element_type=F32)
+            sums[j % 2] = res if j < 2 else sums[j % 2] + res
+        res = sums[0] + sums[1]
+        gi[other[0]] = res[:, :LANES] + res[:, LANES:]
         gb[...] = bias
 
     each(0, once, first_rows)
@@ -398,8 +410,6 @@
             gi[q] = res[:, :LANES] + res[:, LANES:]
         each(0, once, run)
 
-    mine = (c, 2 + c)
-    other = (1 - c, 3 - c)
     to_core = [remote(gi.at[other[i]], rs_r.at[i], send.at[26 + i], rs_sem.at[i], {"smp": core}) for i in range(2)]
     to_x = [remote(rs_s.at[i], rs_r.at[2 + i], send.at[19 + i], rs_sem.at[2 + i], {"smp": across}) for i in range(2)]
     share = [remote(gall.at[mine[i]], gall.at[mine[i]], send.at[21 + 7 * i], ag_sem.at[i], {"smp": core})
@@ -407,22 +417,23 @@
     shared = [remote(gall.at[other[i]], gall.at[other[i]], send.at[21 + 7 * i], ag_sem.at[i], {"smp": core})
               for i in range(2)]
     to_core[0].start()
-    image(other[1])
-    to_core[1].start()
     b1s[...] = row_of(gb[...].T)
     off = v3s[...] - mean
     m1s[...] = row_of(off * off)
     ex_b1.start()
     b1[q_me] = b1s[...]
+    image(mine[0])
     to_core[0].wait_recv()
     rs_s[0] = gi[mine[0]] + rs_r[0]
     to_x[0].start()
+    ex_m1.start()
+    m1[plane] = m1s[...]
+    image(other[1])
+    to_core[1].start()
     image(mine[1])
     to_core[1].wait_recv()
     rs_s[1] = gi[mine[1]] + rs_r[1]
     to_x[1].start()
-    ex_m1.start()
-    m1[plane] = m1s[...]
     ex_v3.drain()
     ex_p3.drain()
     ex_n2.wait()
@@ -437,7 +448,7 @@
 
     def quarter(q, first=False):
         transposed(gall, q)
-        each(0, 2, lambda i: values(wide, i, nz, 2 if first else None, block(q, height), not first))
+        each(0, once, lambda i: values(0, nz, nz, 2 if first else None, block(q, height), not first))
 
     to_x[0].wait_recv()
     gall[mine[0]] = rs_s[0] + rs_r[2]
@@ -445,12 +456,6 @@
     quarter(mine[0], True)
     shared[0].wait_recv()
     quarter(other[0])
-    to_x[1].wait_recv()
-    gall[mine[1]] = rs_s[1] + rs_r[3]
-    share[1].start()
-    ex_gz.start()
-    gown[:, lane(z)] = gall[q_me, block(z), :]
-
     ex_b2.wait()
     ex_m1.wait()
     for k in range(nz):
@@ -460,6 +465,12 @@
     image_b = gb[:8, :]
     curvature = total(added([m1[k] for k in range(4 * ng)])) * inv + F32(LAMBDA) * norm0
     alpha0 = norm0 / curvature
+    to_x[1].wait_recv()
+    gall[mine[1]] = rs_s[1] + rs_r[3]
+    share[1].start()
+    ex_gz.start()
+    gown[:, lane(z)] = gall[q_me, block(z), :]
+
     res_b = fb[...] - alpha0 * (image_b * inv + F32(LAMBDA) * fb[...])
     own_f = fc[q_me]
     res_w = own_f - alpha0 * (gall[q_me] * inv + F32(LAMBDA) * own_f)

time: 82.9 us -> 80.5 us (0.971)
  Pallas kernels: 79.3 us -> 76.9 us
    pallas_call x1, Pallas kernels: 79.3 us -> 76.9 us  [call(): pl.pallas_call(functools.partial(kernel, ng, nz, count), out_shape=(jax.S...]
where the time goes in v4:
time: 80.5 us; the launch traced here: 80.4 us
  Pallas kernels  76.9 us (96%)
  local copies, waits for them, and re-layouts  2.85 us (4%)
    pallas_call x1, Pallas kernels, call(): pl.pallas_call(functools.partial(kernel, ng, nz, count), out_shape=(jax.S...  76.9 us
    unnamed x2, local copies, waits for them, and re-layouts  2.85 us

profile of v4, /device:TPU:1, one launch (start us, length us, event | category | flops | bytes accessed | tf_op | source)
XLA Modules:
  0.0 80.4 jit_solution(8037223525815636310)
XLA Ops:
  0.6 76.9 %step.1 = (f32[32,1024]{1,0:T(8,128)}, f32[8,128]{1,0:T(8,128)}) custom-call(s32[32,1024]{1,0:T(8,128)} %spk_h.1, bf16[1024,1024]{1,0:T(8,128)(2,1)} %w_h.1, f32[8,128]{1,0:T(8,128)} %bitcast.3, f32[32,1024]{1,0:T(8,128)} %fw_h.1, f32[8,128]{1,0:T(8,128)} %bitcast.4), custom_call_target="tpu_custom_call" | custom-call | tf_op jit(solution)/shard_map/step/pallas_call | solution.py:575
  77.5 1.6 %copy.9 = f32[32,1024]{1,0:T(8,128)} copy(f32[32,1024]{1,0:T(8,128)} %get-tuple-element.8) | data formatting | bytes 262144
  79.1 1.3 %copy.10 = f32[1024]{0:T(1024)} copy(f32[1024]{0:T(1024)} %bitcast.5) | data formatting | bytes 8192

commit v5 on v4

--- a/solution.py
+++ b/solution.py
@@ -584,6 +584,31 @@
     )(spk, w, hb, fw, fb)
 
 
+def hand_over(w_in, b_in, w_out, b_out, w, b, sem):
+    loads = [pltpu.make_async_copy(w_in, w, sem.at[0]), pltpu.make_async_copy(b_in, b, sem.at[1])]
+    stores = [pltpu.make_async_copy(w, w_out, sem.at[2]), pltpu.make_async_copy(b, b_out, sem.at[3])]
+    for load in loads:
+        load.start()
+    for load, store in zip(loads, stores):
+        load.wait()
+        store.start()
+    for store in stores:
+        store.wait()
+
+
+def final(w, b):
+    anywhere = pl.BlockSpec(memory_space=pl.ANY)
+    return pl.pallas_call(
+        hand_over,
+        out_shape=(jax.ShapeDtypeStruct(w.shape, F32), jax.ShapeDtypeStruct(b.shape, F32)),
+        in_specs=[anywhere, anywhere],
+        out_specs=(anywhere, anywhere),
+        scratch_shapes=[pltpu.VMEM(w.shape, F32), pltpu.VMEM(b.shape, F32), pltpu.SemaphoreType.DMA((4,))],
+        compiler_params=pltpu.CompilerParams(vmem_limit_bytes=60 * 1024 * 1024),
+        name="hand_over",
+    )(w, b)
+
+
 def solution(mesh):
     ng, ns = mesh.shape["grp"], mesh.shape["smp"]
     nz = ns // 4
@@ -593,7 +618,7 @@
         tile = (8, LANES)
         pad = 8 * LANES - hb.shape[0]
         hb, fb = (jnp.pad(v, (0, pad)).reshape(tile) for v in (hb, fb))
-        out_w, out_b = call(ng, nz, count, spk, w, hb, fw, fb)
+        out_w, out_b = final(*call(ng, nz, count, spk, w, hb, fw, fb))
         return out_w, out_b.reshape(-1)[: nz * LANES]
 
     return jax.shard_map(body, mesh=mesh,

time: 80.5 us -> 79.4 us (0.986)
  local copies, waits for them, and re-layouts: 2.85 us -> 0 us
  Pallas kernels: 76.9 us -> 78.5 us
    unnamed x2 -> x0, local copies, waits for them, and re-layouts: 2.85 us -> none
    pallas_call x0 -> x1, Pallas kernels: none -> 1.6 us  [final(): pl.pallas_call(hand_over, out_shape=(jax.ShapeDtypeStruct(w.shape, F32),...]
where the time goes in v5:
time: 79.4 us; the launch traced here: 79.3 us
  Pallas kernels  78.5 us (99%)
  between operations  0.8 us (1%)
    pallas_call x1, Pallas kernels, call(): pl.pallas_call(functools.partial(kernel, ng, nz, count), out_shape=(jax.S...  76.9 us
    pallas_call x1, Pallas kernels, final(): pl.pallas_call(hand_over, out_shape=(jax.ShapeDtypeStruct(w.shape, F32),...  1.6 us

profile of v5, /device:TPU:1, one launch (start us, length us, event | category | flops | bytes accessed | tf_op | source)
XLA Modules:
  0.0 79.3 jit_solution(4136519881535915627)
XLA Ops:
  0.6 76.9 %step.1 = (f32[32,1024]{1,0:T(8,128)}, f32[8,128]{1,0:T(8,128)}) custom-call(s32[32,1024]{1,0:T(8,128)} %spk_h.1, bf16[1024,1024]{1,0:T(8,128)(2,1)} %w_h.1, f32[8,128]{1,0:T(8,128)} %bitcast.3, f32[32,1024]{1,0:T(8,128)} %fw_h.1, f32[8,128]{1,0:T(8,128)} %bitcast.4), custom_call_target="tpu_custom_call" | custom-call | tf_op jit(solution)/shard_map/step/pallas_call | solution.py:575
  77.5 1.6 %hand_over.1 = (f32[32,1024]{1,0:T(8,128)}, f32[8,128]{1,0:T(8,128)}) custom-call(f32[32,1024]{1,0:T(8,128)} %get-tuple-element.6.w_in, f32[8,128]{1,0:T(8,128)} %get-tuple-element.7.b_in), custom_call_target="tpu_custom_call" | custom-call | tf_op jit(solution)/shard_map/hand_over/pallas_call | solution.py:601

commit v6 on v5

--- a/solution.py
+++ b/solution.py
@@ -145,11 +145,12 @@
 
     loads = [pltpu.make_async_copy(a, b, local_sem.at[i]) for i, (a, b) in enumerate(
         ((spk_h, spk), (w_h.at[:, lane(z)], wv), (hb_h, hb), (fb_h, fb), (fw_h, fw)))]
-    for load in loads:
-        load.start()
     barrier = pltpu.get_barrier_semaphore()
     peers(nz, z, lambda p: pl.semaphore_signal(barrier, inc=1, device_id={"smp": z_index(p)}, device_id_type=MESH))
+    loads[0].start()
     over_all(lambda dev: pl.semaphore_signal(barrier, inc=1, device_id=dev, device_id_type=MESH))
+    for load in loads[1:]:
+        load.start()
 
     ex_v1 = over_grp(lambda p: vbuf.at[p], v1, 1)
     ex_v2 = over_z(lambda p: v2s, v2, 2)
@@ -304,6 +305,9 @@
                 to = (base + k, pl.ds(r, 1), slice(None))
                 vbuf[to] = vbuf[to] + got if more else got
 
+    transposed(fc, q_me)
+    fx[3].wait_recv()
+    transposed(fc, q_core)
     for i in (1, 0):
         from_near[i].wait_recv()
         unpack(pk.at[(down, up)[i]], 2 - i)
@@ -316,9 +320,6 @@
 
     fx[4].wait_recv()
     fx[2].start()
-    fx[3].wait_recv()
-    transposed(fc, q_me)
-    transposed(fc, q_core)
     transposed(fc, q_x)
     early = 3 if nz == 4 else 5
     each(3, early, arrive)

time: 79.4 us -> 79.4 us (level)
  no operation moved by 1% of the time
where the time goes in v6:
time: 79.4 us; the launch traced here: 79.3 us
  Pallas kernels  78.5 us (99%)
  between operations  0.8 us (1%)
    pallas_call x1, Pallas kernels, call(): pl.pallas_call(functools.partial(kernel, ng, nz, count), out_shape=(jax.S...  76.9 us
    pallas_call x1, Pallas kernels, final(): pl.pallas_call(hand_over, out_shape=(jax.ShapeDtypeStruct(w.shape, F32),...  1.6 us

profile of v6, /device:TPU:1, one launch (start us, length us, event | category | flops | bytes accessed | tf_op | source)
XLA Modules:
  0.0 79.3 jit_solution(1326198055038444988)
XLA Ops:
  0.6 76.9 %step.1 = (f32[32,1024]{1,0:T(8,128)}, f32[8,128]{1,0:T(8,128)}) custom-call(s32[32,1024]{1,0:T(8,128)} %spk_h.1, bf16[1024,1024]{1,0:T(8,128)(2,1)} %w_h.1, f32[8,128]{1,0:T(8,128)} %bitcast.3, f32[32,1024]{1,0:T(8,128)} %fw_h.1, f32[8,128]{1,0:T(8,128)} %bitcast.4), custom_call_target="tpu_custom_call" | custom-call | tf_op jit(solution)/shard_map/step/pallas_call | solution.py:576
  77.5 1.6 %hand_over.1 = (f32[32,1024]{1,0:T(8,128)}, f32[8,128]{1,0:T(8,128)}) custom-call(f32[32,1024]{1,0:T(8,128)} %get-tuple-element.6.w_in, f32[8,128]{1,0:T(8,128)} %get-tuple-element.7.b_in), custom_call_target="tpu_custom_call" | custom-call | tf_op jit(solution)/shard_map/hand_over/pallas_call | solution.py:602
